TPU v7x, 32 devices: a whole 2x2x4 slice. The times are simulated.
32 devices in a mesh: expert: 8 (over z, x), pair: 4 (over y, core).
Axes of the slice: x: 2, y: 2, z: 4, core: 2. Of those that a mesh axis runs over, the one named last changes fastest.
Arguments:
- tokens: bfloat16 [12288, 2048], P(('expert', 'pair')), may hold values from -6 to 6
- token_ids: int32 [12288], P(('expert', 'pair')), may hold values from 0 to 8191
- table: int32 [8192], replicated, may hold values from 0 to 15
- w_in: bfloat16 [16, 2048, 2048], P('expert', None, 'pair'), may hold values from -0.125 to 0.125
- w_out: bfloat16 [16, 2048, 2048], P('expert', 'pair'), may hold values from -0.125 to 0.125
Outputs:
- mixed: bfloat16 [12288, 2048], P(('expert', 'pair'))
All inputs are finite; a program needn't handle non-finite values.
Results may differ from a plain program's by a relative error of at most 0.0085.
Values may be sent and summed in bfloat16 or wider, within the bound.
No kernel may reach another device: no remote copies, remote signals or barrier semaphores. Data moves between devices by JAX's collectives and lax.ppermute only.
A program may use at most 192 MiB of HBM per device.

v0:
```python
import jax
import jax.numpy as jnp
from jax import lax
from jax.sharding import PartitionSpec as P


def on_device(tokens, token_ids, table, w_in, w_out):
    groups = lax.axis_size("expert")
    exp_local = w_in.shape[0]
    experts = groups * exp_local
    tok_rows, width = tokens.shape
    slots = max(2, 2 * tok_rows // experts)
    quarter = w_out.shape[1]
    chosen = jnp.take(table, token_ids, axis=0)
    expert_hot = (chosen[:, None] == jnp.arange(experts, dtype=jnp.int32)[None, :]).astype(
        jnp.int32
    )
    earlier = jnp.cumsum(expert_hot, axis=0) - expert_hot
    rank_tok = jnp.sum(earlier * expert_hot, axis=1)
    kept = rank_tok < slots
    column = (chosen // exp_local * slots + rank_tok) * exp_local + chosen % exp_local
    placer = (
        (column[:, None] == jnp.arange(experts * slots, dtype=jnp.int32)[None, :]) & kept[:, None]
    ).astype(jnp.bfloat16)
    packed = jnp.einsum("ts,td->sd", placer, tokens, preferred_element_type=jnp.float32).astype(
        jnp.bfloat16
    )
    packed = packed.reshape(groups * slots, exp_local, width)
    arrived = lax.all_to_all(packed, "expert", split_axis=0, concat_axis=0, tiled=True)
    rows = arrived.shape[0]
    hidden = jax.nn.relu(
        jnp.einsum(
            "red,edh->reh",
            arrived,
            lax.all_gather(w_in, "pair", axis=2, tiled=True),
            preferred_element_type=jnp.float32,
        )
    ).astype(jnp.bfloat16)
    total = jnp.zeros((rows, exp_local, width), jnp.float32)
    piece = lax.all_gather(w_out, "pair", axis=1, tiled=True)
    for index in range(piece.shape[1] // quarter):
        cols = lax.dynamic_slice_in_dim(hidden, index * quarter, quarter, 2)
        part = jnp.einsum(
            "reh,ehd->red",
            cols,
            piece[:, index * quarter : (index + 1) * quarter],
            preferred_element_type=jnp.float32,
        ).astype(jnp.bfloat16)
        total = total + lax.optimization_barrier(part).astype(jnp.float32)
    result = total.astype(jnp.bfloat16)
    returned = lax.all_to_all(result, "expert", split_axis=0, concat_axis=0, tiled=True)
    flat = returned.reshape(experts * slots, width)
    return jnp.dot(placer, flat, preferred_element_type=jnp.float32).astype(jnp.bfloat16)


def solution(mesh):
    in_specs = (
        P(("expert", "pair"), None),
        P(("expert", "pair")),
        P(),
        P("expert", None, "pair"),
        P("expert", "pair", None),
    )
    out_specs = P(("expert", "pair"), None)
    return jax.shard_map(
        on_device, mesh=mesh, in_specs=in_specs, out_specs=out_specs, check_vma=False
    )
```

profile of v0, /device:TPU:0, one launch (start us, length us, event | category | flops | bytes accessed | tf_op | source)
XLA Modules:
  0.0 337.7 jit_solution(6098488606454812090)
XLA Ops:
  6.5 0.0 copy-start
  6.5 0.0 copy-start.3
  6.5 0.0 all-gather.3.cloned.1.call-start
  6.5 0.7 all-gather.3.cloned.1.call-update
  7.3 0.0 copy-start.2
  7.3 0.0 all-gather.5.cloned.1.call-start
  7.3 0.7 all-gather.5.cloned.1.call-update
  8.0 0.0 copy-done.3
  8.1 0.0 copy-done.2
  8.1 2.5 gather_fusion
  10.6 0.9 reduce-window.6
  11.5 0.2 slice_reduce_fusion
  11.8 0.1 fusion.49
  11.9 0.0 copy-done
  11.9 3.6 %convolution_convert_fusion = bf16[768,2048]{1,0:T(8,128)(2,1)} fusion(bf16[384,2048]{1,0:T(8,128)(2,1)S(1)} %copy-done, s32[384]{0:T(512)S(1)} %fusion.54, pred[384]{0:T(512)(128)(4,1)S(1)} %broadcast_compare_fusion), kind=kOutput, calls=%fused_computation.11 | convolution fusion | flops 1210122240 | bytes 4720512 | tf_op jit(solution)/shard_map/ts,td->sd/dot_general | solution.py:25
  15.5 4.7 %reshape.67 = bf16[384,2,2048]{2,1,0:T(2,128)(2,1)S(1)} reshape(bf16[768,2048]{1,0:T(8,128)(2,1)} %convolution_convert_fusion) | data formatting | bytes 6291456 | tf_op jit(solution)/shard_map/reshape | solution.py:28
  20.2 78.0 %all_to_all.10 = bf16[384,2,2048]{2,1,0:T(2,128)(2,1)} all-to-all(bf16[384,2,2048]{2,1,0:T(2,128)(2,1)S(1)} %reshape.67), channel_id=1, replica_groups=mesh['expert'=8,'pair'=4] {'expert'}, dimensions={0} | all-to-all | bytes 6291456 | tf_op jit(solution)/shard_map/all_to_all | solution.py:29
  98.2 19.3 %all-gather.3.cloned.1.call-done = bf16[2,2048,2048]{2,1,0:T(8,128)(2,1)} async-done(((bf16[2,2048,512]{2,1,0:T(8,128)(2,1)}), bf16[2,2048,2048]{2,1,0:T(8,128)(2,1)}) %all-gather.3.cloned.1.call-update) | async-done | bytes 16777232 | tf_op jit(solution)/shard_map/all_gather | solution.py:35
  117.6 14.0 %fusion.33 = bf16[384,2,2048]{2,0,1:T(8,128)(2,1)S(1)} fusion(bf16[2,2048,2048]{2,1,0:T(8,128)(2,1)} %all-gather.3.cloned.1.call-done, bf16[384,2,2048]{2,1,0:T(2,128)(2,1)} %all_to_all.10), kind=kOutput, calls=%fused_computation.21 | convolution fusion | flops 6445596672 | bytes 23068672 | tf_op jit(solution)/shard_map/red,edh->reh/dot_general | solution.py:32
  131.6 93.5 %all-gather.5.cloned.1.call-done = bf16[2,2048,2048]{2,1,0:T(8,128)(2,1)} async-done(((bf16[2,512,2048]{2,1,0:T(8,128)(2,1)}), bf16[2,2048,2048]{2,1,0:T(8,128)(2,1)}) %all-gather.5.cloned.1.call-update) | async-done | bytes 16777232 | tf_op jit(solution)/shard_map/all_gather | solution.py:40
  225.0 0.0 copy-start.4
  225.0 4.1 %fusion.30 = bf16[384,2,2048]{2,0,1:T(8,128)(2,1)S(1)} fusion(bf16[2,2048,2048]{2,1,0:T(8,128)(2,1)} %all-gather.5.cloned.1.call-done, bf16[384,2,2048]{2,0,1:T(8,128)(2,1)S(1)} %fusion.33), kind=kOutput, calls=%fused_computation.20 | convolution fusion | flops 1612185600 | bytes 8126464 | tf_op jit(solution)/shard_map/reh,ehd->red/dot_general | solution.py:43
  229.2 4.7 %fusion.27 = bf16[384,2,2048]{2,0,1:T(8,128)(2,1)S(1)} fusion(bf16[2,2048,2048]{2,1,0:T(8,128)(2,1)} %all-gather.5.cloned.1.call-done, bf16[384,2,2048]{2,0,1:T(8,128)(2,1)S(1)} %fusion.33), kind=kOutput, calls=%fused_computation.19 | convolution fusion | flops 1612185600 | bytes 8126464 | tf_op jit(solution)/shard_map/reh,ehd->red/dot_general | solution.py:43
  233.9 0.0 copy-done.4
  233.9 1.8 fusion.24
  235.8 1.8 fusion.21
  237.6 3.2 add_convert_fusion
  240.8 3.2 copy.12
  244.1 76.5 %all_to_all.11 = bf16[384,2,2048]{2,1,0:T(2,128)(2,1)} all-to-all(bf16[384,2,2048]{2,1,0:T(2,128)(2,1)S(1)} %copy.12), channel_id=1, replica_groups=mesh['expert'=8,'pair'=4] {'expert'}, dimensions={0} | all-to-all | bytes 6291456 | tf_op jit(solution)/shard_map/all_to_all | solution.py:51
  320.6 0.0 copy-start.1
  320.6 5.8 %reshape.68 = bf16[768,2048]{1,0:T(8,128)(2,1)} reshape(bf16[384,2,2048]{2,1,0:T(2,128)(2,1)} %all_to_all.11) | data formatting | bytes 6291456 | tf_op jit(solution)/shard_map/reshape | solution.py:52
  326.4 4.5 %convolution_convert_fusion.1 = bf16[384,2048]{1,0:T(8,128)(2,1)} fusion(bf16[768,2048]{1,0:T(8,128)(2,1)} %reshape.68, s32[384]{0:T(512)S(1)} %fusion.54, pred[384]{0:T(512)(128)(4,1)S(1)} %broadcast_compare_fusion), kind=kOutput, calls=%fused_computation.22 | convolution fusion | flops 1209335808 | bytes 4720512 | tf_op jit(solution)/shard_map/dot_general | solution.py:53
  330.9 0.0 copy-done.1
  (7 shorter events, 0.1 us)
Async XLA Ops:
  6.5 5.4 %copy-start = (bf16[384,2048]{1,0:T(8,128)(2,1)S(1)}, bf16[384,2048]{1,0:T(8,128)(2,1)}, u32[]{:S(2)}) copy-start(bf16[384,2048]{1,0:T(8,128)(2,1)} %param.5) | copy-start | bytes 4718596
  6.5 1.5 copy-start.3
  6.5 111.0 %all-gather.3.cloned.1.call-start = ((), (), s32[]{:S(2)}) async-start(), calls=%async_computation.2 | async-start | bytes 20971520 | tf_op jit(solution)/shard_map/all_gather | solution.py:35
  7.3 0.8 copy-start.2
  7.3 217.8 %all-gather.5.cloned.1.call-start = ((), (), s32[]{:S(2)}) async-start(), calls=%async_computation.3 | async-start | bytes 20971520 | tf_op jit(solution)/shard_map/all_gather | solution.py:40
  225.0 8.9 %copy-start.4 = (bf16[2,2048,2048]{2,1,0:T(8,128)(2,1)S(1)}, bf16[2,2048,2048]{2,1,0:T(8,128)(2,1)}, u32[]{:S(2)}) copy-start(bf16[2,2048,2048]{2,1,0:T(8,128)(2,1)} %all-gather.5.cloned.1.call-done) | copy-start | bytes 50331652
  320.6 10.3 %copy-start.1 = (bf16[384,2048]{1,0:T(8,128)(2,1)S(1)}, bf16[384,2048]{1,0:T(8,128)(2,1)}, u32[]{:S(2)}) copy-start(bf16[384,2048]{1,0:T(8,128)(2,1)} %param.5) | copy-start | bytes 4718596
Sparse Core Ops, SparseCore 0:
  8.9 108.6 all-gather.2
  119.1 105.8 all-gather.4
where the time goes:
time: 338 us
  blocking collectives  154 us (46%)
  waiting for transfers between devices  114 us (34%)
  matrix products  34.6 us (10%)
  local copies, waits for them, and re-layouts  16.6 us (5%)
  between operations  13.5 us (4%)
  other arithmetic  4.29 us (1%)
    all_gather x1, waiting for transfers between devices, on_device(): piece = lax.all_gather(w_out, 'pair', axis=1, tiled=True)  93.5 us
    all_to_all x1, blocking collectives, on_device(): lax.all_to_all(packed, 'expert', split_axis=0, concat_axis=0, tiled=True)  78 us
    all_to_all x1, blocking collectives, on_device(): lax.all_to_all(result, 'expert', split_axis=0, concat_axis=0, tiled=True)  76.5 us
    all_gather x1, waiting for transfers between devices, on_device(): lax.all_gather(w_in, 'pair', axis=2, tiled=True)  19.3 us
    dot_general x1, matrix products, on_device(): jnp.einsum('red,edh->reh', arrived, lax.all_gather(w_in, 'pair', axis=2,...  14 us
    dot_general x4, matrix products, on_device(): jnp.einsum('reh,ehd->red', cols, piece[:, index * quarter:(index + 1) * q...  12.5 us
  transfers between devices with their start and end apart: 2, of which 2 were waited for; matrix products, arithmetic and copies ran while one was open for 8% of the time, Pallas kernels for 0%

commit v1 on v0

--- a/solution.py
+++ b/solution.py
@@ -1,23 +1,34 @@
+import functools
+
 import jax
 import jax.numpy as jnp
 from jax import lax
+from jax.experimental import pallas as pl
+from jax.experimental.pallas import tpu as pltpu
 from jax.sharding import PartitionSpec as P
 
 
-def on_device(tokens, token_ids, table, w_in, w_out):
+MIB = 1 << 20
+
+
+def route(token_ids, table, experts, slots):
+    chosen = jnp.take(table, token_ids, axis=0)
+    expert_hot = (chosen[:, None] == jnp.arange(experts, dtype=jnp.int32)[None, :]).astype(
+        jnp.int32
+    )
+    earlier = jnp.cumsum(expert_hot, axis=0) - expert_hot
+    rank_tok = jnp.sum(earlier * expert_hot, axis=1)
+    return chosen, rank_tok, rank_tok < slots
+
+
+def general(tokens, token_ids, table, w_in, w_out):
     groups = lax.axis_size("expert")
     exp_local = w_in.shape[0]
     experts = groups * exp_local
     tok_rows, width = tokens.shape
     slots = max(2, 2 * tok_rows // experts)
     quarter = w_out.shape[1]
-    chosen = jnp.take(table, token_ids, axis=0)
-    expert_hot = (chosen[:, None] == jnp.arange(experts, dtype=jnp.int32)[None, :]).astype(
-        jnp.int32
-    )
-    earlier = jnp.cumsum(expert_hot, axis=0) - expert_hot
-    rank_tok = jnp.sum(earlier * expert_hot, axis=1)
-    kept = rank_tok < slots
+    chosen, rank_tok, kept = route(token_ids, table, experts, slots)
     column = (chosen // exp_local * slots + rank_tok) * exp_local + chosen % exp_local
     placer = (
         (column[:, None] == jnp.arange(experts * slots, dtype=jnp.int32)[None, :]) & kept[:, None]
@@ -46,11 +57,291 @@
             piece[:, index * quarter : (index + 1) * quarter],
             preferred_element_type=jnp.float32,
         ).astype(jnp.bfloat16)
-        total = total + lax.optimization_barrier(part).astype(jnp.float32)
+        total = total + part.astype(jnp.float32)
     result = total.astype(jnp.bfloat16)
     returned = lax.all_to_all(result, "expert", split_axis=0, concat_axis=0, tiled=True)
     flat = returned.reshape(experts * slots, width)
     return jnp.dot(placer, flat, preferred_element_type=jnp.float32).astype(jnp.bfloat16)
+
+
+WHOLE = pl.BlockSpec(memory_space=pltpu.VMEM)
+
+
+def cost(flops, moved):
+    return pl.CostEstimate(flops=flops, bytes_accessed=moved, transcendentals=0)
+
+
+def write_blocks(ks, per, col_row, tok_ref, outs):
+    tok_rows = tok_ref.shape[0]
+    row = lax.broadcasted_iota(jnp.int32, (per, tok_rows), 0)
+    col = jnp.broadcast_to(col_row, (per, tok_rows))
+    one = jnp.concatenate([(col == row + k * per).astype(jnp.float32) for k in ks], axis=0)
+    got = jnp.dot(one.astype(jnp.bfloat16), tok_ref[...], preferred_element_type=jnp.float32)
+    for i, out in enumerate(outs):
+        out[...] = got[i * per : (i + 1) * per].astype(jnp.bfloat16)
+
+
+def route_kernel(ks, local, slots, me_ref, ids_ref, table_hbm, tok_hbm, row_ref, col_ref, tok_ref, *refs):
+    outs, (table_ref, sems) = refs[: len(ks)], refs[len(ks) :]
+    table_copy = pltpu.make_async_copy(table_hbm, table_ref, sems.at[0])
+    tok_copy = pltpu.make_async_copy(tok_hbm, tok_ref, sems.at[1])
+    table_copy.start()
+    tok_copy.start()
+    tok_rows = tok_ref.shape[0]
+    lines, lanes = table_ref.shape
+    shift = lanes.bit_length() - 1
+    first = lax.broadcasted_iota(jnp.int32, (tok_rows, tok_rows), 0)
+    second = lax.broadcasted_iota(jnp.int32, (tok_rows, tok_rows), 1)
+    same = first == second
+    ids_row = jnp.concatenate([ids_ref[i : i + 1, :] for i in range(ids_ref.shape[0])], axis=1)
+    wide_ids = jnp.broadcast_to(ids_row.astype(jnp.float32), (tok_rows, tok_rows))
+    ids = jnp.sum(jnp.where(same, wide_ids, 0.0), axis=1, keepdims=True).astype(jnp.int32)
+    line = lax.broadcasted_iota(jnp.int32, (tok_rows, lines), 1)
+    lane = lax.broadcasted_iota(jnp.int32, (tok_rows, lanes), 1)
+    hot = (line == jnp.right_shift(ids, shift)).astype(jnp.float32).astype(jnp.bfloat16)
+    table_copy.wait()
+    table = table_ref[...].astype(jnp.float32).astype(jnp.bfloat16)
+    found = jnp.dot(hot, table, preferred_element_type=jnp.float32)
+    found = jnp.where(lane == jnp.bitwise_and(ids, lanes - 1), found, 0.0)
+    chosen = jnp.sum(found, axis=1, keepdims=True).astype(jnp.int32)
+    mine = lane == chosen
+    before = (second < first).astype(jnp.float32).astype(jnp.bfloat16)
+    earlier = jnp.dot(
+        before, mine.astype(jnp.float32).astype(jnp.bfloat16), preferred_element_type=jnp.float32
+    )
+    rank = jnp.sum(jnp.where(mine, earlier, 0.0), axis=1, keepdims=True).astype(jnp.int32)
+    offset = jnp.bitwise_xor(jnp.right_shift(chosen, local.bit_length() - 1), me_ref[0])
+    inner = jnp.bitwise_and(chosen, local - 1)
+    col = jnp.where(rank < slots, (offset * local + inner) * slots + rank, -1)
+    col_ref[...] = col
+    spread = jnp.where(same, col.astype(jnp.float32), 0.0)
+    col_row = jnp.sum(spread, axis=0, keepdims=True).astype(jnp.int32)
+    row_ref[...] = col_row
+    tok_copy.wait()
+    write_blocks(ks, local * slots, col_row, tok_ref, outs)
+
+
+def route_pack(ks, local, slots, me, token_ids, table, tokens):
+    tok_rows, width = tokens.shape
+    per = local * slots
+    lanes = 128
+    lined = table.reshape(-1, lanes)
+    blocks = [jax.ShapeDtypeStruct((per, width), jnp.bfloat16) for _ in ks]
+    there = pl.BlockSpec(memory_space=pltpu.HBM)
+    row, col, tok, *out = pl.pallas_call(
+        functools.partial(route_kernel, ks, local, slots),
+        in_specs=[pl.BlockSpec(memory_space=pltpu.SMEM), WHOLE, there, there],
+        out_specs=[WHOLE] * (3 + len(ks)),
+        out_shape=[
+            jax.ShapeDtypeStruct((1, tok_rows), jnp.int32),
+            jax.ShapeDtypeStruct((tok_rows, 1), jnp.int32),
+            jax.ShapeDtypeStruct(tokens.shape, jnp.bfloat16),
+        ]
+        + blocks,
+        scratch_shapes=[
+            pltpu.VMEM(lined.shape, jnp.int32),
+            pltpu.SemaphoreType.DMA((2,)),
+        ],
+        compiler_params=pltpu.CompilerParams(vmem_limit_bytes=30 * MIB),
+        cost_estimate=cost(4 * len(ks) * per * tok_rows * width, 4 * width * tok_rows),
+        name="route_pack",
+    )(me.reshape(1), token_ids.reshape(-1, lanes), lined, tokens)
+    return row, col, tok, out
+
+
+def pack_kernel(ks, per, row_ref, tok_ref, *outs):
+    write_blocks(ks, per, row_ref[...], tok_ref, outs)
+
+
+def pack(ks, per, row, tokens):
+    tok_rows, width = tokens.shape
+    return pl.pallas_call(
+        functools.partial(pack_kernel, ks, per),
+        in_specs=[WHOLE, WHOLE],
+        out_specs=[WHOLE] * len(ks),
+        out_shape=[jax.ShapeDtypeStruct((per, width), jnp.bfloat16) for _ in ks],
+        compiler_params=pltpu.CompilerParams(vmem_limit_bytes=8 * MIB),
+        cost_estimate=cost(2 * len(ks) * per * tok_rows * width, 4 * width * tok_rows),
+        name="pack",
+    )(row, tokens)
+
+
+def unpack_kernel(ks, per, tile, has_prev, col_ref, *refs):
+    blocks, out = refs[: len(ks)], refs[-1]
+    tok_rows = col_ref.shape[0]
+    cut = pl.ds(pl.multiple_of(pl.program_id(0) * tile, tile), tile)
+    lane = lax.broadcasted_iota(jnp.int32, (tok_rows, per), 1)
+    col = jnp.broadcast_to(col_ref[...], (tok_rows, per))
+    one = jnp.concatenate([(col == lane + k * per).astype(jnp.float32) for k in ks], axis=1)
+    acc = jnp.dot(
+        one.astype(jnp.bfloat16),
+        jnp.concatenate([b[:, cut] for b in blocks], axis=0),
+        preferred_element_type=jnp.float32,
+    )
+    if has_prev:
+        acc = acc + refs[len(ks)][:, cut].astype(jnp.float32)
+    out[...] = acc.astype(jnp.bfloat16)
+
+
+def unpack(ks, per, col, blocks, prev):
+    tok_rows, width = col.shape[0], blocks[0].shape[1]
+    last = prev is not None
+    tile = 1024 if last else width
+    extra = [prev] if last else []
+    return pl.pallas_call(
+        functools.partial(unpack_kernel, ks, per, tile, last),
+        grid=(width // tile,),
+        in_specs=[WHOLE] * (1 + len(ks) + len(extra)),
+        out_specs=pl.BlockSpec((tok_rows, tile), lambda n: (0, n)) if last else WHOLE,
+        out_shape=jax.ShapeDtypeStruct((tok_rows, width), jnp.bfloat16),
+        compiler_params=pltpu.CompilerParams(vmem_limit_bytes=12 * MIB),
+        cost_estimate=cost(2 * len(ks) * per * tok_rows * width, 4 * width * tok_rows),
+        name="unpack",
+    )(col, *blocks, *extra)
+
+
+def add_kernel(a, b, out):
+    out[...] = (a[...].astype(jnp.float32) + b[...].astype(jnp.float32)).astype(jnp.bfloat16)
+
+
+def add(a, b):
+    return pl.pallas_call(
+        add_kernel,
+        in_specs=[WHOLE, WHOLE],
+        out_specs=WHOLE,
+        out_shape=jax.ShapeDtypeStruct(a.shape, jnp.bfloat16),
+        compiler_params=pltpu.CompilerParams(vmem_limit_bytes=4 * MIB),
+        cost_estimate=cost(a.size, 6 * a.size),
+        name="add",
+    )(a, b)
+
+
+def experts_kernel(count, slots, tile, wia, wib, woa, wob, *refs):
+    blocks, outs, x, h = refs[:count], refs[count : 2 * count], refs[-2], refs[-1]
+    local, width, quarter = wia.shape
+    for e in range(local):
+        for i, b in enumerate(blocks):
+            x[i * slots : (i + 1) * slots, :] = b[e]
+        for q, w in enumerate((wia, wib)):
+            g = jnp.dot(x[...], w[e], preferred_element_type=jnp.float32)
+            h[:, q * quarter : (q + 1) * quarter] = jnp.maximum(g, 0.0).astype(jnp.bfloat16)
+
+        def column(t, carry, e=e):
+            c = pl.ds(pl.multiple_of(t * tile, tile), tile)
+            o = jnp.dot(h[:, :quarter], woa[e, :, c], preferred_element_type=jnp.float32)
+            o += jnp.dot(h[:, quarter:], wob[e, :, c], preferred_element_type=jnp.float32)
+            o = o.astype(jnp.bfloat16)
+            for i, out in enumerate(outs):
+                out[e, :, c] = o[i * slots : (i + 1) * slots]
+            return carry
+
+        lax.fori_loop(0, width // tile, column, 0)
+
+
+def experts_call(blocks, weights):
+    local, width, quarter = weights[0].shape
+    slots = blocks[0].shape[1]
+    rows = len(blocks) * slots
+    return pl.pallas_call(
+        functools.partial(experts_kernel, len(blocks), slots, min(1024, width)),
+        in_specs=[WHOLE] * (4 + len(blocks)),
+        out_specs=[WHOLE] * len(blocks),
+        out_shape=[jax.ShapeDtypeStruct(blocks[0].shape, jnp.bfloat16) for _ in blocks],
+        scratch_shapes=[
+            pltpu.VMEM((rows, width), jnp.bfloat16),
+            pltpu.VMEM((rows, 2 * quarter), jnp.bfloat16),
+        ],
+        compiler_params=pltpu.CompilerParams(vmem_limit_bytes=16 * MIB),
+        cost_estimate=cost(
+            8 * local * rows * width * quarter, 2 * local * (4 * width * quarter + 2 * rows * width)
+        ),
+        name="experts",
+    )(*weights, *blocks)
+
+
+def hold_kernel(a, b, x, y, sems):
+    copies = [pltpu.make_async_copy(a, x, sems.at[0]), pltpu.make_async_copy(b, y, sems.at[1])]
+    for copy in copies:
+        copy.start()
+    for copy in copies:
+        copy.wait()
+
+
+def hold(a, b):
+    there = pl.BlockSpec(memory_space=pl.ANY)
+    return pl.pallas_call(
+        hold_kernel,
+        in_specs=[there, there],
+        out_specs=[WHOLE, WHOLE],
+        out_shape=[jax.ShapeDtypeStruct(v.shape, v.dtype) for v in (a, b)],
+        scratch_shapes=[pltpu.SemaphoreType.DMA((2,))],
+        compiler_params=pltpu.CompilerParams(vmem_limit_bytes=4 * MIB),
+        cost_estimate=cost(0, 4 * (a.size + b.size)),
+        name="hold",
+    )(a, b)
+
+
+FIRST, LATER = (2, 4, 1, 0), (3, 5, 6, 7)
+NEAR = ()
+SETS = {"EA": (0, 1), "EB": (2, 3), "EC": (4, 5), "ED": (6, 7)}
+OUT_FIRST, OUT_LATER = (2, 3, 4, 5), (0, 1, 6, 7)
+
+
+def pipelined(tokens, token_ids, table, w_in, w_out):
+    groups, pairs = lax.axis_size("expert"), lax.axis_size("pair")
+    local = w_in.shape[0]
+    tok_rows, width = tokens.shape
+    slots = max(2, 2 * tok_rows // (groups * local))
+    per = local * slots
+    far = pairs // 2
+
+    def to_group(block, k):
+        if k == 0:
+            return block
+        return lax.ppermute(block, "expert", [(g, g ^ k) for g in range(groups)])
+
+    def to_half(block):
+        return lax.ppermute(block, "pair", [(p, (p + far) % pairs) for p in range(pairs)])
+
+    def to_core(block):
+        return lax.ppermute(block, "pair", [(p, p ^ 1) for p in range(pairs)])
+
+    theirs_in, theirs_out = to_core(w_in), to_core(w_out)
+    theirs_in, theirs_out = hold(theirs_in, theirs_out)
+    weights = (w_in, theirs_in, w_out, theirs_out)
+    me = lax.axis_index("expert").astype(jnp.int32)
+    row, col, tok, out = route_pack(FIRST, local, slots, me, token_ids, table, tokens)
+    packed = dict(zip(FIRST, out))
+    packed.update(zip(LATER, pack(LATER, per, row, tok)))
+    here = {k: to_group(packed[k], k) for k in range(groups)}
+    there = {}
+    for k in range(groups):
+        if k in NEAR:
+            there[k] = to_group(to_half(packed[k]), k)
+        else:
+            there[k] = to_half(here[k])
+    home = {}
+    for ks in SETS.values():
+        blocks = [b[k].reshape(local, slots, width) for b in (there, here) for k in ks]
+        parts = [p.reshape(per, width) for p in experts_call(blocks, weights)]
+        for k, theirs, ours in zip(ks, parts[: len(ks)], parts[len(ks) :]):
+            back = to_half(theirs)
+            home[k] = to_group(add(ours, back), k)
+    part = unpack(OUT_FIRST, per, col, [home[k] for k in OUT_FIRST], None)
+    return unpack(OUT_LATER, per, col, [home[k] for k in OUT_LATER], part)
+
+
+def on_device(tokens, token_ids, table, w_in, w_out):
+    groups, pairs = lax.axis_size("expert"), lax.axis_size("pair")
+    local, _, quarter = w_in.shape
+    tok_rows, width = tokens.shape
+    slots = max(2, 2 * tok_rows // (groups * local))
+    fits = groups == 8 and pairs == 4 and local & (local - 1) == 0 and groups * local <= 128
+    fits = fits and slots % 16 == 0 and tok_rows % 128 == 0 and table.shape[0] % 1024 == 0
+    fits = fits and width % 1024 == 0 and quarter % 256 == 0
+    if not fits:
+        return general(tokens, token_ids, table, w_in, w_out)
+    return pipelined(tokens, token_ids, table, w_in, w_out)
 
 
 def solution(mesh):

time: 338 us -> 232 us (0.69)
  the two profiles are of different devices: /device:TPU:0 before, /device:TPU:8 now
where the time goes in v1:
time: 232 us
  waiting for transfers between devices  153 us (66%)
  starting transfers between devices  47 us (20%)
  Pallas kernels  28.2 us (12%)
  local copies, waits for them, and re-layouts  2.85 us (1%)
    ppermute x14, waiting for transfers between devices, to_group(): return lax.ppermute(block, 'expert', [(g, g ^ k) for g in range(groups)])  86.2 us
    ppermute x16, waiting for transfers between devices, to_half(): lax.ppermute(block, 'pair', [(p, (p + far) % pairs) for p in range(pairs)])  67.2 us
    ppermute x14, starting transfers between devices, to_group(): return lax.ppermute(block, 'expert', [(g, g ^ k) for g in range(groups)])  32.2 us
    pallas_call x4, Pallas kernels, experts_call(): pl.pallas_call(functools.partial(experts_kernel, len(blocks), slots, min(...  17.5 us
    ppermute x16, starting transfers between devices, to_half(): lax.ppermute(block, 'pair', [(p, (p + far) % pairs) for p in range(pairs)])  14.3 us
  transfers between devices with their start and end apart: 32, of which 22 were waited for; matrix products, arithmetic and copies ran while one was open for 0% of the time, Pallas kernels for 11%

profile of v1, /device:TPU:8, one launch (start us, length us, event | category | flops | bytes accessed | tf_op | source)
XLA Modules:
  0.0 231.7 jit_solution(6506096479305495830)
XLA Ops:
  0.0 0.5 collective-permute-start.1
  0.5 1.4 copy-done.2
  1.9 0.8 copy-done.3
  2.7 0.7 copy-done.4
  3.4 1.8 route_pack.1
  5.2 1.6 collective-permute-start.2
  6.8 1.5 collective-permute-start.3
  8.3 1.0 pack.1
  9.2 1.6 collective-permute-start.8
  10.9 5.4 %collective-permute-done.2 = bf16[96,2048]{1,0:T(8,128)(2,1)S(1)} collective-permute-done((bf16[96,2048]{1,0:T(8,128)(2,1)S(1)}, bf16[96,2048]{1,0:T(8,128)(2,1)S(1)}, u32[]{:S(2)}, u32[]{:S(2)}) %collective-permute-start.2) | collective-permute-done | bytes 393248 | tf_op jit(solution)/shard_map/ppermute | solution.py:304
  16.3 0.2 collective-permute-start.16
  16.5 1.0 collective-permute-done.3
  17.5 1.7 collective-permute-start.18
  19.2 9.0 %collective-permute-done.8 = bf16[96,2048]{1,0:T(8,128)(2,1)S(1)} collective-permute-done((bf16[96,2048]{1,0:T(8,128)(2,1)S(1)}, bf16[96,2048]{1,0:T(8,128)(2,1)S(1)}, u32[]{:S(2)}, u32[]{:S(2)}) %collective-permute-start.8) | collective-permute-done | bytes 393248 | tf_op jit(solution)/shard_map/ppermute | solution.py:301
  28.2 3.5 %collective-permute-done.16 = bf16[96,2048]{1,0:T(8,128)(2,1)S(1)} collective-permute-done((bf16[96,2048]{1,0:T(8,128)(2,1)S(1)}, bf16[96,2048]{1,0:T(8,128)(2,1)S(1)}, u32[]{:S(2)}, u32[]{:S(2)}) %collective-permute-start.16) | collective-permute-done | bytes 393248 | tf_op jit(solution)/shard_map/ppermute | solution.py:301
  31.7 9.6 %collective-permute-start.26 = (bf16[96,2048]{1,0:T(8,128)(2,1)S(1)}, bf16[96,2048]{1,0:T(8,128)(2,1)S(1)}, u32[]{:S(2)}, u32[]{:S(2)}) collective-permute-start(bf16[96,2048]{1,0:T(8,128)(2,1)S(1)} %get-tuple-element.58), channel_id=1, source_target_pairs={{0,20},{4,16},{8,28},{12,24},{16,4},{20,0},{24,12},{28,8},{1,21},{... | collective-permute-start | bytes 1179656 | tf_op jit(solution)/shard_map/ppermute | solution.py:301
  41.4 3.6 %collective-permute-done.18 = bf16[96,2048]{1,0:T(8,128)(2,1)S(1)} collective-permute-done((bf16[96,2048]{1,0:T(8,128)(2,1)S(1)}, bf16[96,2048]{1,0:T(8,128)(2,1)S(1)}, u32[]{:S(2)}, u32[]{:S(2)}) %collective-permute-start.18) | collective-permute-done | bytes 393248 | tf_op jit(solution)/shard_map/ppermute | solution.py:301
  44.9 0.5 collective-permute-start.4
  45.4 2.1 collective-permute-done.24
  47.5 2.7 %collective-permute-start.10 = (bf16[96,2048]{1,0:T(8,128)(2,1)S(1)}, bf16[96,2048]{1,0:T(8,128)(2,1)S(1)}, u32[]{:S(2)}, u32[]{:S(2)}) collective-permute-start(bf16[96,2048]{1,0:T(8,128)(2,1)S(1)} %get-tuple-element.46), channel_id=1, source_target_pairs={{0,28},{4,24},{8,20},{12,16},{16,12},{20,8},{24,4},{28,0},{1,29},{... | collective-permute-start | bytes 1179656 | tf_op jit(solution)/shard_map/ppermute | solution.py:301
  50.1 0.5 collective-permute-start.17
  50.7 1.5 collective-permute-start.19
  52.2 3.5 %hold.1 = (bf16[2,2048,512]{2,1,0:T(8,128)(2,1)S(1)}, bf16[2,512,2048]{2,1,0:T(8,128)(2,1)S(1)}) custom-call(bf16[2,2048,512]{2,1,0:T(8,128)(2,1)} %collective-permute-done.a, bf16[2,512,2048]{2,1,0:T(8,128)(2,1)} %collective-permute-done.1.b), custom_call_target="tpu_custom_call" | custom-call | bytes 16777216 | tf_op jit(solution)/shard_map/hold/pallas_call | solution.py:272
  55.7 15.8 %collective-permute-done.26 = bf16[96,2048]{1,0:T(8,128)(2,1)S(1)} collective-permute-done((bf16[96,2048]{1,0:T(8,128)(2,1)S(1)}, bf16[96,2048]{1,0:T(8,128)(2,1)S(1)}, u32[]{:S(2)}, u32[]{:S(2)}) %collective-permute-start.26) | collective-permute-done | bytes 393248 | tf_op jit(solution)/shard_map/ppermute | solution.py:301
  71.5 0.5 collective-permute-start.25
  72.0 1.5 collective-permute-start.27
  73.5 4.3 %experts.4 = (bf16[2,48,2048]{2,1,0:T(8,128)(2,1)S(1)}, bf16[2,48,2048]{2,1,0:T(8,128)(2,1)S(1)}, bf16[2,48,2048]{2,1,0:T(8,128)(2,1)S(1)}, bf16[2,48,2048]{2,1,0:T(8,128)(2,1)S(1)}) custom-call(bf16[2,2048,512]{2,1,0:T(8,128)(2,1)S(1)} %copy-done, bf16[2,2048,512]{2,1,0:T(8,128)(2,1)S(1)} %get-tuple-element.35.wib, bf16[2,512,2048]{2,1,0:T(8,128)(2,1)S(1)} %copy-done.1, ...), custom_call_target="tpu_custom_call" | custom-call | flops 3221225472 | bytes 19922944 | tf_op jit(solution)/shard_map/experts/pallas_call | solution.py:245
  77.9 1.9 collective-permute-done.10
  79.8 0.5 collective-permute-start.9
  80.3 1.5 collective-permute-start.11
  81.9 0.5 collective-permute-start.6
  82.4 4.3 %experts.6 = (bf16[2,48,2048]{2,1,0:T(8,128)(2,1)S(1)}, bf16[2,48,2048]{2,1,0:T(8,128)(2,1)S(1)}, bf16[2,48,2048]{2,1,0:T(8,128)(2,1)S(1)}, bf16[2,48,2048]{2,1,0:T(8,128)(2,1)S(1)}) custom-call(bf16[2,2048,512]{2,1,0:T(8,128)(2,1)S(1)} %copy-done, bf16[2,2048,512]{2,1,0:T(8,128)(2,1)S(1)} %get-tuple-element.35.wib, bf16[2,512,2048]{2,1,0:T(8,128)(2,1)S(1)} %copy-done.1, ...), custom_call_target="tpu_custom_call" | custom-call | flops 3221225472 | bytes 19922944 | tf_op jit(solution)/shard_map/experts/pallas_call | solution.py:245
  86.7 1.6 collective-permute-start.20
  88.3 3.6 %collective-permute-done.27 = bf16[96,2048]{1,0:T(8,128)(2,1)S(1)} collective-permute-done((bf16[96,2048]{1,0:T(8,128)(2,1)S(1)}, bf16[96,2048]{1,0:T(8,128)(2,1)S(1)}, u32[]{:S(2)}, u32[]{:S(2)}) %collective-permute-start.27) | collective-permute-done | bytes 393248 | tf_op jit(solution)/shard_map/ppermute | solution.py:304
  91.9 0.5 collective-permute-start.22
  92.4 4.3 %experts.7 = (bf16[2,48,2048]{2,1,0:T(8,128)(2,1)S(1)}, bf16[2,48,2048]{2,1,0:T(8,128)(2,1)S(1)}, bf16[2,48,2048]{2,1,0:T(8,128)(2,1)S(1)}, bf16[2,48,2048]{2,1,0:T(8,128)(2,1)S(1)}) custom-call(bf16[2,2048,512]{2,1,0:T(8,128)(2,1)S(1)} %copy-done, bf16[2,2048,512]{2,1,0:T(8,128)(2,1)S(1)} %get-tuple-element.35.wib, bf16[2,512,2048]{2,1,0:T(8,128)(2,1)S(1)} %copy-done.1, ...), custom_call_target="tpu_custom_call" | custom-call | flops 3221225472 | bytes 19922944 | tf_op jit(solution)/shard_map/experts/pallas_call | solution.py:245
  96.7 3.6 %collective-permute-done.9 = bf16[96,2048]{1,0:T(8,128)(2,1)S(1)} collective-permute-done((bf16[96,2048]{1,0:T(8,128)(2,1)S(1)}, bf16[96,2048]{1,0:T(8,128)(2,1)S(1)}, u32[]{:S(2)}, u32[]{:S(2)}) %collective-permute-start.9) | collective-permute-done | bytes 393248 | tf_op jit(solution)/shard_map/ppermute | solution.py:304
  100.3 0.5 collective-permute-start.28
  100.8 7.9 %collective-permute-done.11 = bf16[96,2048]{1,0:T(8,128)(2,1)S(1)} collective-permute-done((bf16[96,2048]{1,0:T(8,128)(2,1)S(1)}, bf16[96,2048]{1,0:T(8,128)(2,1)S(1)}, u32[]{:S(2)}, u32[]{:S(2)}) %collective-permute-start.11) | collective-permute-done | bytes 393248 | tf_op jit(solution)/shard_map/ppermute | solution.py:304
  108.8 0.5 collective-permute-start.30
  109.3 4.5 %experts.5 = (bf16[2,48,2048]{2,1,0:T(8,128)(2,1)S(1)}, bf16[2,48,2048]{2,1,0:T(8,128)(2,1)S(1)}, bf16[2,48,2048]{2,1,0:T(8,128)(2,1)S(1)}, bf16[2,48,2048]{2,1,0:T(8,128)(2,1)S(1)}) custom-call(bf16[2,2048,512]{2,1,0:T(8,128)(2,1)S(1)} %copy-done, bf16[2,2048,512]{2,1,0:T(8,128)(2,1)S(1)} %get-tuple-element.35.wib, bf16[2,512,2048]{2,1,0:T(8,128)(2,1)S(1)} %copy-done.1, ...), custom_call_target="tpu_custom_call" | custom-call | flops 3221225472 | bytes 19922944 | tf_op jit(solution)/shard_map/experts/pallas_call | solution.py:245
  113.8 11.8 %collective-permute-done.20.b = bf16[96,2048]{1,0:T(8,128)(2,1)S(1)} collective-permute-done((bf16[96,2048]{1,0:T(8,128)(2,1)S(1)}, bf16[96,2048]{1,0:T(8,128)(2,1)S(1)}, u32[]{:S(2)}, u32[]{:S(2)}) %collective-permute-start.20) | collective-permute-done | bytes 393248 | tf_op jit(solution)/shard_map/ppermute | solution.py:304
  125.6 0.5 collective-permute-start.12
  126.1 7.9 %collective-permute-done.22.b = bf16[96,2048]{1,0:T(8,128)(2,1)S(1)} collective-permute-done((bf16[96,2048]{1,0:T(8,128)(2,1)S(1)}, bf16[96,2048]{1,0:T(8,128)(2,1)S(1)}, u32[]{:S(2)}, u32[]{:S(2)}) %collective-permute-start.22) | collective-permute-done | bytes 393248 | tf_op jit(solution)/shard_map/ppermute | solution.py:304
  134.0 0.5 collective-permute-start.14
  134.7 1.6 collective-permute-start.5
  136.3 6.1 %collective-permute-done.28.b = bf16[96,2048]{1,0:T(8,128)(2,1)S(1)} collective-permute-done((bf16[96,2048]{1,0:T(8,128)(2,1)S(1)}, bf16[96,2048]{1,0:T(8,128)(2,1)S(1)}, u32[]{:S(2)}, u32[]{:S(2)}) %collective-permute-start.28) | collective-permute-done | bytes 393248 | tf_op jit(solution)/shard_map/ppermute | solution.py:304
  142.5 1.4 collective-permute-start.21
  143.9 7.0 %collective-permute-done.30.b = bf16[96,2048]{1,0:T(8,128)(2,1)S(1)} collective-permute-done((bf16[96,2048]{1,0:T(8,128)(2,1)S(1)}, bf16[96,2048]{1,0:T(8,128)(2,1)S(1)}, u32[]{:S(2)}, u32[]{:S(2)}) %collective-permute-start.30) | collective-permute-done | bytes 393248 | tf_op jit(solution)/shard_map/ppermute | solution.py:304
  150.9 2.3 %collective-permute-start.23 = (bf16[96,2048]{1,0:T(8,128)(2,1)S(1)}, bf16[96,2048]{1,0:T(8,128)(2,1)S(1)}, u32[]{:S(2)}, u32[]{:S(2)}) collective-permute-start(bf16[96,2048]{1,0:T(8,128)(2,1)S(1)} %add.13), channel_id=1, source_target_pairs={{0,12},{4,8},{8,4},{12,0},{16,28},{20,24},{24,20},{28,16},{1,13},{... | collective-permute-start | bytes 1179656 | tf_op jit(solution)/shard_map/ppermute | solution.py:301
  153.4 5.9 %collective-permute-done.12.b = bf16[96,2048]{1,0:T(8,128)(2,1)S(1)} collective-permute-done((bf16[96,2048]{1,0:T(8,128)(2,1)S(1)}, bf16[96,2048]{1,0:T(8,128)(2,1)S(1)}, u32[]{:S(2)}, u32[]{:S(2)}) %collective-permute-start.12) | collective-permute-done | bytes 393248 | tf_op jit(solution)/shard_map/ppermute | solution.py:304
  159.3 3.3 %collective-permute-start.29 = (bf16[96,2048]{1,0:T(8,128)(2,1)S(1)}, bf16[96,2048]{1,0:T(8,128)(2,1)S(1)}, u32[]{:S(2)}, u32[]{:S(2)}) collective-permute-start(bf16[96,2048]{1,0:T(8,128)(2,1)S(1)} %add.14), channel_id=1, source_target_pairs={{0,16},{4,20},{8,24},{12,28},{16,0},{20,4},{24,8},{28,12},{1,17},{... | collective-permute-start | bytes 1179656 | tf_op jit(solution)/shard_map/ppermute | solution.py:301
  162.7 5.1 %collective-permute-done.14.b = bf16[96,2048]{1,0:T(8,128)(2,1)S(1)} collective-permute-done((bf16[96,2048]{1,0:T(8,128)(2,1)S(1)}, bf16[96,2048]{1,0:T(8,128)(2,1)S(1)}, u32[]{:S(2)}, u32[]{:S(2)}) %collective-permute-start.14) | collective-permute-done | bytes 393248 | tf_op jit(solution)/shard_map/ppermute | solution.py:304
  167.7 4.3 %collective-permute-start.31 = (bf16[96,2048]{1,0:T(8,128)(2,1)S(1)}, bf16[96,2048]{1,0:T(8,128)(2,1)S(1)}, u32[]{:S(2)}, u32[]{:S(2)}) collective-permute-start(bf16[96,2048]{1,0:T(8,128)(2,1)S(1)} %add.15), channel_id=1, source_target_pairs={{0,20},{4,16},{8,28},{12,24},{16,4},{20,0},{24,12},{28,8},{1,21},{... | collective-permute-start | bytes 1179656 | tf_op jit(solution)/shard_map/ppermute | solution.py:301
  172.3 2.8 %collective-permute-done.5.b = bf16[96,2048]{1,0:T(8,128)(2,1)S(1)} collective-permute-done((bf16[96,2048]{1,0:T(8,128)(2,1)S(1)}, bf16[96,2048]{1,0:T(8,128)(2,1)S(1)}, u32[]{:S(2)}, u32[]{:S(2)}) %collective-permute-start.5) | collective-permute-done | bytes 393248 | tf_op jit(solution)/shard_map/ppermute | solution.py:304
  175.1 0.5 collective-permute-start.7
  175.7 1.4 collective-permute-start.13
  177.1 1.5 collective-permute-start.15
  178.7 23.6 %collective-permute-done.29.refs_2_ = bf16[96,2048]{1,0:T(8,128)(2,1)S(1)} collective-permute-done((bf16[96,2048]{1,0:T(8,128)(2,1)S(1)}, bf16[96,2048]{1,0:T(8,128)(2,1)S(1)}, u32[]{:S(2)}, u32[]{:S(2)}) %collective-permute-start.29) | collective-permute-done | bytes 393248 | tf_op jit(solution)/shard_map/ppermute | solution.py:301
  202.3 8.4 %collective-permute-done.31.refs_3_ = bf16[96,2048]{1,0:T(8,128)(2,1)S(1)} collective-permute-done((bf16[96,2048]{1,0:T(8,128)(2,1)S(1)}, bf16[96,2048]{1,0:T(8,128)(2,1)S(1)}, u32[]{:S(2)}, u32[]{:S(2)}) %collective-permute-start.31) | collective-permute-done | bytes 393248 | tf_op jit(solution)/shard_map/ppermute | solution.py:301
  210.7 1.2 unpack.2.refs_4_
  211.9 8.7 %collective-permute-done.13.refs_2_ = bf16[96,2048]{1,0:T(8,128)(2,1)S(1)} collective-permute-done((bf16[96,2048]{1,0:T(8,128)(2,1)S(1)}, bf16[96,2048]{1,0:T(8,128)(2,1)S(1)}, u32[]{:S(2)}, u32[]{:S(2)}) %collective-permute-start.13) | collective-permute-done | bytes 393248 | tf_op jit(solution)/shard_map/ppermute | solution.py:301
  220.6 8.6 %collective-permute-done.15.refs_3_ = bf16[96,2048]{1,0:T(8,128)(2,1)S(1)} collective-permute-done((bf16[96,2048]{1,0:T(8,128)(2,1)S(1)}, bf16[96,2048]{1,0:T(8,128)(2,1)S(1)}, u32[]{:S(2)}, u32[]{:S(2)}) %collective-permute-start.15) | collective-permute-done | bytes 393248 | tf_op jit(solution)/shard_map/ppermute | solution.py:301
  229.2 2.4 %unpack.3 = bf16[384,2048]{1,0:T(8,128)(2,1)} custom-call(s32[384,1]{1,0:T(8,128)S(1)} %get-tuple-element.34.col_ref, bf16[96,2048]{1,0:T(8,128)(2,1)S(1)} %add.8.refs_0_, bf16[96,2048]{1,0:T(8,128)(2,1)S(1)} %collective-permute-done.7.refs_1_, bf16[96,2048]{1,0:T(8,128)(2,1)S(1)} %collective-permute-done.13.refs_2_, ...), custom_call_target="tpu_custom_call" | custom-call | flops 603979776 | bytes 3145728 | tf_op jit(solution)/shard_map/unpack/pallas_call | solution.py:191
  (27 shorter events, 0.8 us)
Async XLA Ops:
  0.0 50.1 %collective-permute-start = (bf16[2,2048,512]{2,1,0:T(8,128)(2,1)}, bf16[2,2048,512]{2,1,0:T(8,128)(2,1)}, u32[]{:S(2)}, u32[]{:S(2)}) collective-permute-start(bf16[2,2048,512]{2,1,0:T(8,128)(2,1)} %wia.7), channel_id=1, source_target_pairs={{0,1},{1,0},{2,3},{3,2},{4,5},{5,4},{6,7},{7,6},{8,9},{9,8},{10,11... | collective-permute-start | bytes 12582920 | tf_op jit(solution)/shard_map/ppermute | solution.py:307
  0.0 50.7 %collective-permute-start.1 = (bf16[2,512,2048]{2,1,0:T(8,128)(2,1)}, bf16[2,512,2048]{2,1,0:T(8,128)(2,1)}, u32[]{:S(2)}, u32[]{:S(2)}) collective-permute-start(bf16[2,512,2048]{2,1,0:T(8,128)(2,1)} %woa.7), channel_id=1, source_target_pairs={{0,1},{1,0},{2,3},{3,2},{4,5},{5,4},{6,7},{7,6},{8,9},{9,8},{10,11... | collective-permute-start | bytes 12582920 | tf_op jit(solution)/shard_map/ppermute | solution.py:307
  0.5 1.4 copy-start.2
  1.9 0.8 copy-start.3
  2.7 0.7 copy-start.4
  5.2 11.1 %collective-permute-start.2 = (bf16[96,2048]{1,0:T(8,128)(2,1)S(1)}, bf16[96,2048]{1,0:T(8,128)(2,1)S(1)}, u32[]{:S(2)}, u32[]{:S(2)}) collective-permute-start(bf16[96,2048]{1,0:T(8,128)(2,1)S(1)} %get-tuple-element.37), channel_id=1, source_target_pairs={{0,2},{1,3},{2,0},{3,1},{4,6},{5,7},{6,4},{7,5},{8,10},{9,11},{10,... | collective-permute-start | bytes 1179656 | tf_op jit(solution)/shard_map/ppermute | solution.py:304
  6.8 10.7 %collective-permute-start.3 = (bf16[96,2048]{1,0:T(8,128)(2,1)S(1)}, bf16[96,2048]{1,0:T(8,128)(2,1)S(1)}, u32[]{:S(2)}, u32[]{:S(2)}) collective-permute-start(bf16[96,2048]{1,0:T(8,128)(2,1)S(1)} %get-tuple-element.38), channel_id=1, source_target_pairs={{0,4},{4,0},{8,12},{12,8},{16,20},{20,16},{24,28},{28,24},{1,5},{5... | collective-permute-start | bytes 1179656 | tf_op jit(solution)/shard_map/ppermute | solution.py:301
  9.2 19.0 %collective-permute-start.8 = (bf16[96,2048]{1,0:T(8,128)(2,1)S(1)}, bf16[96,2048]{1,0:T(8,128)(2,1)S(1)}, u32[]{:S(2)}, u32[]{:S(2)}) collective-permute-start(bf16[96,2048]{1,0:T(8,128)(2,1)S(1)} %get-tuple-element.45), channel_id=1, source_target_pairs={{0,24},{4,28},{8,16},{12,20},{16,8},{20,12},{24,0},{28,4},{1,25},{... | collective-permute-start | bytes 1179656 | tf_op jit(solution)/shard_map/ppermute | solution.py:301
  16.3 15.5 %collective-permute-start.16 = (bf16[96,2048]{1,0:T(8,128)(2,1)S(1)}, bf16[96,2048]{1,0:T(8,128)(2,1)S(1)}, u32[]{:S(2)}, u32[]{:S(2)}) collective-permute-start(bf16[96,2048]{1,0:T(8,128)(2,1)S(1)} %get-tuple-element.51), channel_id=1, source_target_pairs={{0,8},{4,12},{8,0},{12,4},{16,24},{20,28},{24,16},{28,20},{1,9},{5... | collective-permute-start | bytes 1179656 | tf_op jit(solution)/shard_map/ppermute | solution.py:301
  17.5 27.4 %collective-permute-start.18 = (bf16[96,2048]{1,0:T(8,128)(2,1)S(1)}, bf16[96,2048]{1,0:T(8,128)(2,1)S(1)}, u32[]{:S(2)}, u32[]{:S(2)}) collective-permute-start(bf16[96,2048]{1,0:T(8,128)(2,1)S(1)} %get-tuple-element.52), channel_id=1, source_target_pairs={{0,12},{4,8},{8,4},{12,0},{16,28},{20,24},{24,20},{28,16},{1,13},{... | collective-permute-start | bytes 1179656 | tf_op jit(solution)/shard_map/ppermute | solution.py:301
  28.2 19.3 %collective-permute-start.24 = (bf16[96,2048]{1,0:T(8,128)(2,1)S(1)}, bf16[96,2048]{1,0:T(8,128)(2,1)S(1)}, u32[]{:S(2)}, u32[]{:S(2)}) collective-permute-start(bf16[96,2048]{1,0:T(8,128)(2,1)S(1)} %get-tuple-element.57), channel_id=1, source_target_pairs={{0,16},{4,20},{8,24},{12,28},{16,0},{20,4},{24,8},{28,12},{1,17},{... | collective-permute-start | bytes 1179656 | tf_op jit(solution)/shard_map/ppermute | solution.py:301
  31.7 39.7 %collective-permute-start.26 = (bf16[96,2048]{1,0:T(8,128)(2,1)S(1)}, bf16[96,2048]{1,0:T(8,128)(2,1)S(1)}, u32[]{:S(2)}, u32[]{:S(2)}) collective-permute-start(bf16[96,2048]{1,0:T(8,128)(2,1)S(1)} %get-tuple-element.58), channel_id=1, source_target_pairs={{0,20},{4,16},{8,28},{12,24},{16,4},{20,0},{24,12},{28,8},{1,21},{... | collective-permute-start | bytes 1179656 | tf_op jit(solution)/shard_map/ppermute | solution.py:301
  44.9 27.1 %collective-permute-start.4 = (bf16[96,2048]{1,0:T(8,128)(2,1)S(1)}, bf16[96,2048]{1,0:T(8,128)(2,1)S(1)}, u32[]{:S(2)}, u32[]{:S(2)}) collective-permute-start(bf16[96,2048]{1,0:T(8,128)(2,1)S(1)} %collective-permute-done.3), channel_id=1, source_target_pairs={{0,2},{1,3},{2,0},{3,1},{4,6},{5,7},{6,4},{7,5},{8,10},{9,11},{10,... | collective-permute-start | bytes 1179656 | tf_op jit(solution)/shard_map/ppermute | solution.py:304
  47.5 26.1 %copy-start = (bf16[2,2048,512]{2,1,0:T(8,128)(2,1)S(1)}, bf16[2,2048,512]{2,1,0:T(8,128)(2,1)}, u32[]{:S(2)}) copy-start(bf16[2,2048,512]{2,1,0:T(8,128)(2,1)} %wia.7) | copy-start | bytes 12582916
  47.5 26.1 %copy-start.1 = (bf16[2,512,2048]{2,1,0:T(8,128)(2,1)S(1)}, bf16[2,512,2048]{2,1,0:T(8,128)(2,1)}, u32[]{:S(2)}) copy-start(bf16[2,512,2048]{2,1,0:T(8,128)(2,1)} %woa.7) | copy-start | bytes 12582916
  47.5 32.4 %collective-permute-start.10 = (bf16[96,2048]{1,0:T(8,128)(2,1)S(1)}, bf16[96,2048]{1,0:T(8,128)(2,1)S(1)}, u32[]{:S(2)}, u32[]{:S(2)}) collective-permute-start(bf16[96,2048]{1,0:T(8,128)(2,1)S(1)} %get-tuple-element.46), channel_id=1, source_target_pairs={{0,28},{4,24},{8,20},{12,16},{16,12},{20,8},{24,4},{28,0},{1,29},{... | collective-permute-start | bytes 1179656 | tf_op jit(solution)/shard_map/ppermute | solution.py:301
  50.1 30.2 %collective-permute-start.17 = (bf16[96,2048]{1,0:T(8,128)(2,1)S(1)}, bf16[96,2048]{1,0:T(8,128)(2,1)S(1)}, u32[]{:S(2)}, u32[]{:S(2)}) collective-permute-start(bf16[96,2048]{1,0:T(8,128)(2,1)S(1)} %collective-permute-done.16), channel_id=1, source_target_pairs={{0,2},{1,3},{2,0},{3,1},{4,6},{5,7},{6,4},{7,5},{8,10},{9,11},{10,... | collective-permute-start | bytes 1179656 | tf_op jit(solution)/shard_map/ppermute | solution.py:304
  50.7 31.2 %collective-permute-start.19 = (bf16[96,2048]{1,0:T(8,128)(2,1)S(1)}, bf16[96,2048]{1,0:T(8,128)(2,1)S(1)}, u32[]{:S(2)}, u32[]{:S(2)}) collective-permute-start(bf16[96,2048]{1,0:T(8,128)(2,1)S(1)} %collective-permute-done.18), channel_id=1, source_target_pairs={{0,2},{1,3},{2,0},{3,1},{4,6},{5,7},{6,4},{7,5},{8,10},{9,11},{10,... | collective-permute-start | bytes 1179656 | tf_op jit(solution)/shard_map/ppermute | solution.py:304
  71.5 15.2 %collective-permute-start.25 = (bf16[96,2048]{1,0:T(8,128)(2,1)S(1)}, bf16[96,2048]{1,0:T(8,128)(2,1)S(1)}, u32[]{:S(2)}, u32[]{:S(2)}) collective-permute-start(bf16[96,2048]{1,0:T(8,128)(2,1)S(1)} %collective-permute-done.24), channel_id=1, source_target_pairs={{0,2},{1,3},{2,0},{3,1},{4,6},{5,7},{6,4},{7,5},{8,10},{9,11},{10,... | collective-permute-start | bytes 1179656 | tf_op jit(solution)/shard_map/ppermute | solution.py:304
  72.0 19.9 %collective-permute-start.27 = (bf16[96,2048]{1,0:T(8,128)(2,1)S(1)}, bf16[96,2048]{1,0:T(8,128)(2,1)S(1)}, u32[]{:S(2)}, u32[]{:S(2)}) collective-permute-start(bf16[96,2048]{1,0:T(8,128)(2,1)S(1)} %collective-permute-done.26), channel_id=1, source_target_pairs={{0,2},{1,3},{2,0},{3,1},{4,6},{5,7},{6,4},{7,5},{8,10},{9,11},{10,... | collective-permute-start | bytes 1179656 | tf_op jit(solution)/shard_map/ppermute | solution.py:304
  79.8 20.5 %collective-permute-start.9 = (bf16[96,2048]{1,0:T(8,128)(2,1)S(1)}, bf16[96,2048]{1,0:T(8,128)(2,1)S(1)}, u32[]{:S(2)}, u32[]{:S(2)}) collective-permute-start(bf16[96,2048]{1,0:T(8,128)(2,1)S(1)} %collective-permute-done.8), channel_id=1, source_target_pairs={{0,2},{1,3},{2,0},{3,1},{4,6},{5,7},{6,4},{7,5},{8,10},{9,11},{10,... | collective-permute-start | bytes 1179656 | tf_op jit(solution)/shard_map/ppermute | solution.py:304
  80.3 28.4 %collective-permute-start.11 = (bf16[96,2048]{1,0:T(8,128)(2,1)S(1)}, bf16[96,2048]{1,0:T(8,128)(2,1)S(1)}, u32[]{:S(2)}, u32[]{:S(2)}) collective-permute-start(bf16[96,2048]{1,0:T(8,128)(2,1)S(1)} %collective-permute-done.10), channel_id=1, source_target_pairs={{0,2},{1,3},{2,0},{3,1},{4,6},{5,7},{6,4},{7,5},{8,10},{9,11},{10,... | collective-permute-start | bytes 1179656 | tf_op jit(solution)/shard_map/ppermute | solution.py:304
  81.9 52.9 %collective-permute-start.6 = (bf16[96,2048]{1,0:T(8,128)(2,1)S(1)}, bf16[96,2048]{1,0:T(8,128)(2,1)S(1)}, u32[]{:S(2)}, u32[]{:S(2)}) collective-permute-start(bf16[96,2048]{1,0:T(8,128)(2,1)S(1)} %bitcast.60), channel_id=1, source_target_pairs={{0,2},{1,3},{2,0},{3,1},{4,6},{5,7},{6,4},{7,5},{8,10},{9,11},{10,... | collective-permute-start | bytes 1179656 | tf_op jit(solution)/shard_map/ppermute | solution.py:304
  86.7 38.9 %collective-permute-start.20 = (bf16[96,2048]{1,0:T(8,128)(2,1)S(1)}, bf16[96,2048]{1,0:T(8,128)(2,1)S(1)}, u32[]{:S(2)}, u32[]{:S(2)}) collective-permute-start(bf16[96,2048]{1,0:T(8,128)(2,1)S(1)} %bitcast.66), channel_id=1, source_target_pairs={{0,2},{1,3},{2,0},{3,1},{4,6},{5,7},{6,4},{7,5},{8,10},{9,11},{10,... | collective-permute-start | bytes 1179656 | tf_op jit(solution)/shard_map/ppermute | solution.py:304
  91.9 42.1 %collective-permute-start.22 = (bf16[96,2048]{1,0:T(8,128)(2,1)S(1)}, bf16[96,2048]{1,0:T(8,128)(2,1)S(1)}, u32[]{:S(2)}, u32[]{:S(2)}) collective-permute-start(bf16[96,2048]{1,0:T(8,128)(2,1)S(1)} %bitcast.65), channel_id=1, source_target_pairs={{0,2},{1,3},{2,0},{3,1},{4,6},{5,7},{6,4},{7,5},{8,10},{9,11},{10,... | collective-permute-start | bytes 1179656 | tf_op jit(solution)/shard_map/ppermute | solution.py:304
  100.3 42.1 %collective-permute-start.28 = (bf16[96,2048]{1,0:T(8,128)(2,1)S(1)}, bf16[96,2048]{1,0:T(8,128)(2,1)S(1)}, u32[]{:S(2)}, u32[]{:S(2)}) collective-permute-start(bf16[96,2048]{1,0:T(8,128)(2,1)S(1)} %bitcast.63), channel_id=1, source_target_pairs={{0,2},{1,3},{2,0},{3,1},{4,6},{5,7},{6,4},{7,5},{8,10},{9,11},{10,... | collective-permute-start | bytes 1179656 | tf_op jit(solution)/shard_map/ppermute | solution.py:304
  108.8 42.1 %collective-permute-start.30 = (bf16[96,2048]{1,0:T(8,128)(2,1)S(1)}, bf16[96,2048]{1,0:T(8,128)(2,1)S(1)}, u32[]{:S(2)}, u32[]{:S(2)}) collective-permute-start(bf16[96,2048]{1,0:T(8,128)(2,1)S(1)} %bitcast.61), channel_id=1, source_target_pairs={{0,2},{1,3},{2,0},{3,1},{4,6},{5,7},{6,4},{7,5},{8,10},{9,11},{10,... | collective-permute-start | bytes 1179656 | tf_op jit(solution)/shard_map/ppermute | solution.py:304
  125.6 33.7 %collective-permute-start.12 = (bf16[96,2048]{1,0:T(8,128)(2,1)S(1)}, bf16[96,2048]{1,0:T(8,128)(2,1)S(1)}, u32[]{:S(2)}, u32[]{:S(2)}) collective-permute-start(bf16[96,2048]{1,0:T(8,128)(2,1)S(1)} %bitcast.64), channel_id=1, source_target_pairs={{0,2},{1,3},{2,0},{3,1},{4,6},{5,7},{6,4},{7,5},{8,10},{9,11},{10,... | collective-permute-start | bytes 1179656 | tf_op jit(solution)/shard_map/ppermute | solution.py:304
  134.0 33.7 %collective-permute-start.14 = (bf16[96,2048]{1,0:T(8,128)(2,1)S(1)}, bf16[96,2048]{1,0:T(8,128)(2,1)S(1)}, u32[]{:S(2)}, u32[]{:S(2)}) collective-permute-start(bf16[96,2048]{1,0:T(8,128)(2,1)S(1)} %bitcast.62), channel_id=1, source_target_pairs={{0,2},{1,3},{2,0},{3,1},{4,6},{5,7},{6,4},{7,5},{8,10},{9,11},{10,... | collective-permute-start | bytes 1179656 | tf_op jit(solution)/shard_map/ppermute | solution.py:304
  134.7 40.4 %collective-permute-start.5 = (bf16[96,2048]{1,0:T(8,128)(2,1)S(1)}, bf16[96,2048]{1,0:T(8,128)(2,1)S(1)}, u32[]{:S(2)}, u32[]{:S(2)}) collective-permute-start(bf16[96,2048]{1,0:T(8,128)(2,1)S(1)} %bitcast.59), channel_id=1, source_target_pairs={{0,2},{1,3},{2,0},{3,1},{4,6},{5,7},{6,4},{7,5},{8,10},{9,11},{10,... | collective-permute-start | bytes 1179656 | tf_op jit(solution)/shard_map/ppermute | solution.py:304
  142.5 33.2 %collective-permute-start.21 = (bf16[96,2048]{1,0:T(8,128)(2,1)S(1)}, bf16[96,2048]{1,0:T(8,128)(2,1)S(1)}, u32[]{:S(2)}, u32[]{:S(2)}) collective-permute-start(bf16[96,2048]{1,0:T(8,128)(2,1)S(1)} %add.12), channel_id=1, source_target_pairs={{0,8},{4,12},{8,0},{12,4},{16,24},{20,28},{24,16},{28,20},{1,9},{5... | collective-permute-start | bytes 1179656 | tf_op jit(solution)/shard_map/ppermute | solution.py:301
  150.9 26.2 %collective-permute-start.23 = (bf16[96,2048]{1,0:T(8,128)(2,1)S(1)}, bf16[96,2048]{1,0:T(8,128)(2,1)S(1)}, u32[]{:S(2)}, u32[]{:S(2)}) collective-permute-start(bf16[96,2048]{1,0:T(8,128)(2,1)S(1)} %add.13), channel_id=1, source_target_pairs={{0,12},{4,8},{8,4},{12,0},{16,28},{20,24},{24,20},{28,16},{1,13},{... | collective-permute-start | bytes 1179656 | tf_op jit(solution)/shard_map/ppermute | solution.py:301
  159.3 43.0 %collective-permute-start.29 = (bf16[96,2048]{1,0:T(8,128)(2,1)S(1)}, bf16[96,2048]{1,0:T(8,128)(2,1)S(1)}, u32[]{:S(2)}, u32[]{:S(2)}) collective-permute-start(bf16[96,2048]{1,0:T(8,128)(2,1)S(1)} %add.14), channel_id=1, source_target_pairs={{0,16},{4,20},{8,24},{12,28},{16,0},{20,4},{24,8},{28,12},{1,17},{... | collective-permute-start | bytes 1179656 | tf_op jit(solution)/shard_map/ppermute | solution.py:301
  167.7 43.0 %collective-permute-start.31 = (bf16[96,2048]{1,0:T(8,128)(2,1)S(1)}, bf16[96,2048]{1,0:T(8,128)(2,1)S(1)}, u32[]{:S(2)}, u32[]{:S(2)}) collective-permute-start(bf16[96,2048]{1,0:T(8,128)(2,1)S(1)} %add.15), channel_id=1, source_target_pairs={{0,20},{4,16},{8,28},{12,24},{16,4},{20,0},{24,12},{28,8},{1,21},{... | collective-permute-start | bytes 1179656 | tf_op jit(solution)/shard_map/ppermute | solution.py:301
  175.1 36.8 %collective-permute-start.7 = (bf16[96,2048]{1,0:T(8,128)(2,1)S(1)}, bf16[96,2048]{1,0:T(8,128)(2,1)S(1)}, u32[]{:S(2)}, u32[]{:S(2)}) collective-permute-start(bf16[96,2048]{1,0:T(8,128)(2,1)S(1)} %add.9), channel_id=1, source_target_pairs={{0,4},{4,0},{8,12},{12,8},{16,20},{20,16},{24,28},{28,24},{1,5},{5... | collective-permute-start | bytes 1179656 | tf_op jit(solution)/shard_map/ppermute | solution.py:301
  175.7 45.0 %collective-permute-start.13 = (bf16[96,2048]{1,0:T(8,128)(2,1)S(1)}, bf16[96,2048]{1,0:T(8,128)(2,1)S(1)}, u32[]{:S(2)}, u32[]{:S(2)}) collective-permute-start(bf16[96,2048]{1,0:T(8,128)(2,1)S(1)} %add.10), channel_id=1, source_target_pairs={{0,24},{4,28},{8,16},{12,20},{16,8},{20,12},{24,0},{28,4},{1,25},{... | collective-permute-start | bytes 1179656 | tf_op jit(solution)/shard_map/ppermute | solution.py:301
  177.1 52.1 %collective-permute-start.15 = (bf16[96,2048]{1,0:T(8,128)(2,1)S(1)}, bf16[96,2048]{1,0:T(8,128)(2,1)S(1)}, u32[]{:S(2)}, u32[]{:S(2)}) collective-permute-start(bf16[96,2048]{1,0:T(8,128)(2,1)S(1)} %add.11), channel_id=1, source_target_pairs={{0,28},{4,24},{8,20},{12,16},{16,12},{20,8},{24,4},{28,0},{1,29},{... | collective-permute-start | bytes 1179656 | tf_op jit(solution)/shard_map/ppermute | solution.py:301

commit v2 on v1

--- a/solution.py
+++ b/solution.py
@@ -142,7 +142,7 @@
             pltpu.VMEM(lined.shape, jnp.int32),
             pltpu.SemaphoreType.DMA((2,)),
         ],
-        compiler_params=pltpu.CompilerParams(vmem_limit_bytes=30 * MIB),
+        compiler_params=pltpu.CompilerParams(vmem_limit_bytes=50 * MIB),
         cost_estimate=cost(4 * len(ks) * per * tok_rows * width, 4 * width * tok_rows),
         name="route_pack",
     )(me.reshape(1), token_ids.reshape(-1, lanes), lined, tokens)
@@ -166,32 +166,40 @@
     )(row, tokens)
 
 
-def unpack_kernel(ks, per, tile, has_prev, col_ref, *refs):
-    blocks, out = refs[: len(ks)], refs[-1]
+def unpack_kernel(ks, pairs, per, tile, has_prev, col_ref, *refs):
+    single, out = len(ks) - pairs, refs[-1]
+    count = single + 2 * pairs
     tok_rows = col_ref.shape[0]
     cut = pl.ds(pl.multiple_of(pl.program_id(0) * tile, tile), tile)
     lane = lax.broadcasted_iota(jnp.int32, (tok_rows, per), 1)
     col = jnp.broadcast_to(col_ref[...], (tok_rows, per))
     one = jnp.concatenate([(col == lane + k * per).astype(jnp.float32) for k in ks], axis=1)
+    blocks = [b[:, cut] for b in refs[:single]]
+    for i in range(single, count, 2):
+        total = refs[i][:, cut].astype(jnp.float32) + refs[i + 1][:, cut].astype(jnp.float32)
+        blocks.append(total.astype(jnp.bfloat16))
     acc = jnp.dot(
         one.astype(jnp.bfloat16),
-        jnp.concatenate([b[:, cut] for b in blocks], axis=0),
+        jnp.concatenate(blocks, axis=0),
         preferred_element_type=jnp.float32,
     )
     if has_prev:
-        acc = acc + refs[len(ks)][:, cut].astype(jnp.float32)
+        acc = acc + refs[count][:, cut].astype(jnp.float32)
     out[...] = acc.astype(jnp.bfloat16)
 
 
-def unpack(ks, per, col, blocks, prev):
+def unpack(ks, per, col, home, prev):
+    ks = sorted(ks, key=lambda k: len(home[k]))
+    blocks = [b for k in ks for b in home[k]]
+    pairs = len(blocks) - len(ks)
     tok_rows, width = col.shape[0], blocks[0].shape[1]
     last = prev is not None
     tile = 1024 if last else width
     extra = [prev] if last else []
     return pl.pallas_call(
-        functools.partial(unpack_kernel, ks, per, tile, last),
+        functools.partial(unpack_kernel, ks, pairs, per, tile, last),
         grid=(width // tile,),
-        in_specs=[WHOLE] * (1 + len(ks) + len(extra)),
+        in_specs=[WHOLE] * (1 + len(blocks) + len(extra)),
         out_specs=pl.BlockSpec((tok_rows, tile), lambda n: (0, n)) if last else WHOLE,
         out_shape=jax.ShapeDtypeStruct((tok_rows, width), jnp.bfloat16),
         compiler_params=pltpu.CompilerParams(vmem_limit_bytes=12 * MIB),
@@ -283,8 +291,9 @@
 
 FIRST, LATER = (2, 4, 1, 0), (3, 5, 6, 7)
 NEAR = ()
-SETS = {"EA": (0, 1), "EB": (2, 3), "EC": (4, 5), "ED": (6, 7)}
-OUT_FIRST, OUT_LATER = (2, 3, 4, 5), (0, 1, 6, 7)
+LATE = (0, 1)
+SETS = {"EA": (0, 1), "EC": (4, 5), "EB": (2, 6), "ED": (3, 7)}
+OUT_FIRST, OUT_LATER = (2, 3, 4, 5, 6, 7), (0, 1)
 
 
 def pipelined(tokens, token_ids, table, w_in, w_out):
@@ -325,10 +334,13 @@
         blocks = [b[k].reshape(local, slots, width) for b in (there, here) for k in ks]
         parts = [p.reshape(per, width) for p in experts_call(blocks, weights)]
         for k, theirs, ours in zip(ks, parts[: len(ks)], parts[len(ks) :]):
-            back = to_half(theirs)
-            home[k] = to_group(add(ours, back), k)
-    part = unpack(OUT_FIRST, per, col, [home[k] for k in OUT_FIRST], None)
-    return unpack(OUT_LATER, per, col, [home[k] for k in OUT_LATER], part)
+            if k in LATE:
+                back = to_half(to_group(theirs, k))
+                home[k] = (to_group(ours, k), back)
+            else:
+                home[k] = (to_group(add(ours, to_half(theirs)), k),)
+    part = unpack(OUT_FIRST, per, col, home, None)
+    return unpack(OUT_LATER, per, col, home, part)
 
 
 def on_device(tokens, token_ids, table, w_in, w_out):

time: 232 us -> 250 us (1.078)
  the two profiles are of different devices: /device:TPU:8 before, /device:TPU:9 now
where the time goes in v2:
time: 250 us
  waiting for transfers between devices  185 us (74%)
  starting transfers between devices  35.1 us (14%)
  Pallas kernels  28.6 us (11%)
    ppermute x15, waiting for transfers between devices, to_group(): return lax.ppermute(block, 'expert', [(g, g ^ k) for g in range(groups)])  117 us
    ppermute x16, waiting for transfers between devices, to_half(): lax.ppermute(block, 'pair', [(p, (p + far) % pairs) for p in range(pairs)])  67.5 us
    ppermute x15, starting transfers between devices, to_group(): return lax.ppermute(block, 'expert', [(g, g ^ k) for g in range(groups)])  17.7 us
    pallas_call x4, Pallas kernels, experts_call(): pl.pallas_call(functools.partial(experts_kernel, len(blocks), slots, min(...  17.5 us
    ppermute x16, starting transfers between devices, to_half(): lax.ppermute(block, 'pair', [(p, (p + far) % pairs) for p in range(pairs)])  16.7 us
  transfers between devices with their start and end apart: 33, of which 21 were waited for; matrix products, arithmetic and copies ran while one was open for 0% of the time, Pallas kernels for 11%

profile of v2, /device:TPU:9, one launch (start us, length us, event | category | flops | bytes accessed | tf_op | source)
XLA Modules:
  0.0 250.2 jit_solution(491254453183054825)
XLA Ops:
  0.0 0.7 collective-permute-start
  0.7 0.8 copy-done.2
  1.4 0.7 copy-done.3
  2.1 2.4 route_pack.1
  4.6 1.0 pack.1
  5.6 2.6 %collective-permute-start.11 = (bf16[96,2048]{1,0:T(8,128)(2,1)S(1)}, bf16[96,2048]{1,0:T(8,128)(2,1)S(1)}, u32[]{:S(2)}, u32[]{:S(2)}) collective-permute-start(bf16[96,2048]{1,0:T(8,128)(2,1)S(1)} %get-tuple-element.46), channel_id=1, source_target_pairs={{0,24},{4,28},{8,16},{12,20},{16,8},{20,12},{24,0},{28,4},{1,25},{... | collective-permute-start | bytes 1179656 | tf_op jit(solution)/shard_map/ppermute | solution.py:310
  8.3 2.0 collective-permute-start.15
  10.3 4.5 %collective-permute-done.9 = bf16[96,2048]{1,0:T(8,128)(2,1)S(1)} collective-permute-done((bf16[96,2048]{1,0:T(8,128)(2,1)S(1)}, bf16[96,2048]{1,0:T(8,128)(2,1)S(1)}, u32[]{:S(2)}, u32[]{:S(2)}) %collective-permute-start.9) | collective-permute-done | bytes 393248 | tf_op jit(solution)/shard_map/ppermute | solution.py:310
  14.8 2.2 collective-permute-start.17
  17.0 7.5 %collective-permute-done.11 = bf16[96,2048]{1,0:T(8,128)(2,1)S(1)} collective-permute-done((bf16[96,2048]{1,0:T(8,128)(2,1)S(1)}, bf16[96,2048]{1,0:T(8,128)(2,1)S(1)}, u32[]{:S(2)}, u32[]{:S(2)}) %collective-permute-start.11) | collective-permute-done | bytes 393248 | tf_op jit(solution)/shard_map/ppermute | solution.py:310
  24.6 0.8 collective-permute-start.21
  25.4 12.4 %collective-permute-done.15 = bf16[96,2048]{1,0:T(8,128)(2,1)S(1)} collective-permute-done((bf16[96,2048]{1,0:T(8,128)(2,1)S(1)}, bf16[96,2048]{1,0:T(8,128)(2,1)S(1)}, u32[]{:S(2)}, u32[]{:S(2)}) %collective-permute-start.15) | collective-permute-done | bytes 393248 | tf_op jit(solution)/shard_map/ppermute | solution.py:310
  37.8 27.1 %collective-permute-done.17 = bf16[96,2048]{1,0:T(8,128)(2,1)S(1)} collective-permute-done((bf16[96,2048]{1,0:T(8,128)(2,1)S(1)}, bf16[96,2048]{1,0:T(8,128)(2,1)S(1)}, u32[]{:S(2)}, u32[]{:S(2)}) %collective-permute-start.17) | collective-permute-done | bytes 393248 | tf_op jit(solution)/shard_map/ppermute | solution.py:310
  64.9 1.2 collective-permute-start.10
  66.1 3.9 %collective-permute-done.21 = bf16[96,2048]{1,0:T(8,128)(2,1)S(1)} collective-permute-done((bf16[96,2048]{1,0:T(8,128)(2,1)S(1)}, bf16[96,2048]{1,0:T(8,128)(2,1)S(1)}, u32[]{:S(2)}, u32[]{:S(2)}) %collective-permute-start.21) | collective-permute-done | bytes 393248 | tf_op jit(solution)/shard_map/ppermute | solution.py:310
  70.0 1.3 collective-permute-start.12
  71.3 7.2 %collective-permute-done.23 = bf16[96,2048]{1,0:T(8,128)(2,1)S(1)} collective-permute-done((bf16[96,2048]{1,0:T(8,128)(2,1)S(1)}, bf16[96,2048]{1,0:T(8,128)(2,1)S(1)}, u32[]{:S(2)}, u32[]{:S(2)}) %collective-permute-start.23) | collective-permute-done | bytes 393248 | tf_op jit(solution)/shard_map/ppermute | solution.py:310
  78.5 1.7 collective-permute-start.3
  80.2 1.2 collective-permute-start.16
  81.4 0.3 collective-permute-start.18
  81.7 3.5 %hold.1 = (bf16[2,2048,512]{2,1,0:T(8,128)(2,1)S(1)}, bf16[2,512,2048]{2,1,0:T(8,128)(2,1)S(1)}) custom-call(bf16[2,2048,512]{2,1,0:T(8,128)(2,1)} %collective-permute-done.a, bf16[2,512,2048]{2,1,0:T(8,128)(2,1)} %collective-permute-done.1.b), custom_call_target="tpu_custom_call" | custom-call | bytes 16777216 | tf_op jit(solution)/shard_map/hold/pallas_call | solution.py:280
  85.2 1.3 collective-permute-start.22
  86.5 0.3 collective-permute-start.24
  86.7 4.3 %experts.5 = (bf16[2,48,2048]{2,1,0:T(8,128)(2,1)S(1)}, bf16[2,48,2048]{2,1,0:T(8,128)(2,1)S(1)}, bf16[2,48,2048]{2,1,0:T(8,128)(2,1)S(1)}, bf16[2,48,2048]{2,1,0:T(8,128)(2,1)S(1)}) custom-call(bf16[2,2048,512]{2,1,0:T(8,128)(2,1)S(1)} %copy-done, bf16[2,2048,512]{2,1,0:T(8,128)(2,1)S(1)} %get-tuple-element.35.wib, bf16[2,512,2048]{2,1,0:T(8,128)(2,1)S(1)} %copy-done.1, ...), custom_call_target="tpu_custom_call" | custom-call | flops 3221225472 | bytes 19922944 | tf_op jit(solution)/shard_map/experts/pallas_call | solution.py:253
  91.1 1.3 collective-permute-start.2
  92.3 0.3 collective-permute-start.4
  92.6 7.2 %collective-permute-done.18 = bf16[96,2048]{1,0:T(8,128)(2,1)S(1)} collective-permute-done((bf16[96,2048]{1,0:T(8,128)(2,1)S(1)}, bf16[96,2048]{1,0:T(8,128)(2,1)S(1)}, u32[]{:S(2)}, u32[]{:S(2)}) %collective-permute-start.18) | collective-permute-done | bytes 393248 | tf_op jit(solution)/shard_map/ppermute | solution.py:313
  99.8 1.2 collective-permute-start.13
  101.0 4.3 %experts.6 = (bf16[2,48,2048]{2,1,0:T(8,128)(2,1)S(1)}, bf16[2,48,2048]{2,1,0:T(8,128)(2,1)S(1)}, bf16[2,48,2048]{2,1,0:T(8,128)(2,1)S(1)}, bf16[2,48,2048]{2,1,0:T(8,128)(2,1)S(1)}) custom-call(bf16[2,2048,512]{2,1,0:T(8,128)(2,1)S(1)} %copy-done, bf16[2,2048,512]{2,1,0:T(8,128)(2,1)S(1)} %get-tuple-element.35.wib, bf16[2,512,2048]{2,1,0:T(8,128)(2,1)S(1)} %copy-done.1, ...), custom_call_target="tpu_custom_call" | custom-call | flops 3221225472 | bytes 19922944 | tf_op jit(solution)/shard_map/experts/pallas_call | solution.py:253
  105.3 2.9 %collective-permute-done.22 = bf16[96,2048]{1,0:T(8,128)(2,1)S(1)} collective-permute-done((bf16[96,2048]{1,0:T(8,128)(2,1)S(1)}, bf16[96,2048]{1,0:T(8,128)(2,1)S(1)}, u32[]{:S(2)}, u32[]{:S(2)}) %collective-permute-start.22) | collective-permute-done | bytes 393248 | tf_op jit(solution)/shard_map/ppermute | solution.py:313
  108.2 1.2 collective-permute-start.19
  109.4 7.2 %collective-permute-done.24 = bf16[96,2048]{1,0:T(8,128)(2,1)S(1)} collective-permute-done((bf16[96,2048]{1,0:T(8,128)(2,1)S(1)}, bf16[96,2048]{1,0:T(8,128)(2,1)S(1)}, u32[]{:S(2)}, u32[]{:S(2)}) %collective-permute-start.24) | collective-permute-done | bytes 393248 | tf_op jit(solution)/shard_map/ppermute | solution.py:313
  116.6 4.3 %experts.7 = (bf16[2,48,2048]{2,1,0:T(8,128)(2,1)S(1)}, bf16[2,48,2048]{2,1,0:T(8,128)(2,1)S(1)}, bf16[2,48,2048]{2,1,0:T(8,128)(2,1)S(1)}, bf16[2,48,2048]{2,1,0:T(8,128)(2,1)S(1)}) custom-call(bf16[2,2048,512]{2,1,0:T(8,128)(2,1)S(1)} %copy-done, bf16[2,2048,512]{2,1,0:T(8,128)(2,1)S(1)} %get-tuple-element.35.wib, bf16[2,512,2048]{2,1,0:T(8,128)(2,1)S(1)} %copy-done.1, ...), custom_call_target="tpu_custom_call" | custom-call | flops 3221225472 | bytes 19922944 | tf_op jit(solution)/shard_map/experts/pallas_call | solution.py:253
  121.0 1.3 collective-permute-start.25
  122.2 2.8 %collective-permute-done.2 = bf16[96,2048]{1,0:T(8,128)(2,1)S(1)} collective-permute-done((bf16[96,2048]{1,0:T(8,128)(2,1)S(1)}, bf16[96,2048]{1,0:T(8,128)(2,1)S(1)}, u32[]{:S(2)}, u32[]{:S(2)}) %collective-permute-start.2) | collective-permute-done | bytes 393248 | tf_op jit(solution)/shard_map/ppermute | solution.py:313
  125.1 1.2 collective-permute-start.27
  126.3 7.2 %collective-permute-done.4 = bf16[96,2048]{1,0:T(8,128)(2,1)S(1)} collective-permute-done((bf16[96,2048]{1,0:T(8,128)(2,1)S(1)}, bf16[96,2048]{1,0:T(8,128)(2,1)S(1)}, u32[]{:S(2)}, u32[]{:S(2)}) %collective-permute-start.4) | collective-permute-done | bytes 393248 | tf_op jit(solution)/shard_map/ppermute | solution.py:313
  133.5 1.2 collective-permute-start.29
  134.7 7.2 %collective-permute-done.13.b = bf16[96,2048]{1,0:T(8,128)(2,1)S(1)} collective-permute-done((bf16[96,2048]{1,0:T(8,128)(2,1)S(1)}, bf16[96,2048]{1,0:T(8,128)(2,1)S(1)}, u32[]{:S(2)}, u32[]{:S(2)}) %collective-permute-start.13) | collective-permute-done | bytes 393248 | tf_op jit(solution)/shard_map/ppermute | solution.py:313
  141.9 1.2 collective-permute-start.31
  143.1 4.5 %experts.4 = (bf16[2,48,2048]{2,1,0:T(8,128)(2,1)S(1)}, bf16[2,48,2048]{2,1,0:T(8,128)(2,1)S(1)}, bf16[2,48,2048]{2,1,0:T(8,128)(2,1)S(1)}, bf16[2,48,2048]{2,1,0:T(8,128)(2,1)S(1)}) custom-call(bf16[2,2048,512]{2,1,0:T(8,128)(2,1)S(1)} %copy-done, bf16[2,2048,512]{2,1,0:T(8,128)(2,1)S(1)} %get-tuple-element.35.wib, bf16[2,512,2048]{2,1,0:T(8,128)(2,1)S(1)} %copy-done.1, ...), custom_call_target="tpu_custom_call" | custom-call | flops 3221225472 | bytes 19922944 | tf_op jit(solution)/shard_map/experts/pallas_call | solution.py:253
  147.6 0.1 add.6
  147.7 2.6 %collective-permute-done.19.b = bf16[96,2048]{1,0:T(8,128)(2,1)S(1)} collective-permute-done((bf16[96,2048]{1,0:T(8,128)(2,1)S(1)}, bf16[96,2048]{1,0:T(8,128)(2,1)S(1)}, u32[]{:S(2)}, u32[]{:S(2)}) %collective-permute-start.19) | collective-permute-done | bytes 393248 | tf_op jit(solution)/shard_map/ppermute | solution.py:313
  150.4 8.4 %collective-permute-done.25.b = bf16[96,2048]{1,0:T(8,128)(2,1)S(1)} collective-permute-done((bf16[96,2048]{1,0:T(8,128)(2,1)S(1)}, bf16[96,2048]{1,0:T(8,128)(2,1)S(1)}, u32[]{:S(2)}, u32[]{:S(2)}) %collective-permute-start.25) | collective-permute-done | bytes 393248 | tf_op jit(solution)/shard_map/ppermute | solution.py:313
  158.8 0.9 collective-permute-start.14
  159.6 0.1 add.7
  159.7 7.5 %collective-permute-done.27.b = bf16[96,2048]{1,0:T(8,128)(2,1)S(1)} collective-permute-done((bf16[96,2048]{1,0:T(8,128)(2,1)S(1)}, bf16[96,2048]{1,0:T(8,128)(2,1)S(1)}, u32[]{:S(2)}, u32[]{:S(2)}) %collective-permute-start.27) | collective-permute-done | bytes 393248 | tf_op jit(solution)/shard_map/ppermute | solution.py:313
  167.2 1.8 collective-permute-start.20
  169.0 0.1 add.8
  169.1 6.5 %collective-permute-done.29.b = bf16[96,2048]{1,0:T(8,128)(2,1)S(1)} collective-permute-done((bf16[96,2048]{1,0:T(8,128)(2,1)S(1)}, bf16[96,2048]{1,0:T(8,128)(2,1)S(1)}, u32[]{:S(2)}, u32[]{:S(2)}) %collective-permute-start.29) | collective-permute-done | bytes 393248 | tf_op jit(solution)/shard_map/ppermute | solution.py:313
  175.6 0.3 collective-permute-start.26
  176.0 8.0 %collective-permute-done.31.b = bf16[96,2048]{1,0:T(8,128)(2,1)S(1)} collective-permute-done((bf16[96,2048]{1,0:T(8,128)(2,1)S(1)}, bf16[96,2048]{1,0:T(8,128)(2,1)S(1)}, u32[]{:S(2)}, u32[]{:S(2)}) %collective-permute-start.31) | collective-permute-done | bytes 393248 | tf_op jit(solution)/shard_map/ppermute | solution.py:313
  184.0 1.6 collective-permute-start.28
  185.7 0.1 add.11
  185.9 1.4 collective-permute-start.30
  187.3 1.3 collective-permute-start.5
  188.6 28.8 %collective-permute-done.26.refs_2_ = bf16[96,2048]{1,0:T(8,128)(2,1)S(1)} collective-permute-done((bf16[96,2048]{1,0:T(8,128)(2,1)S(1)}, bf16[96,2048]{1,0:T(8,128)(2,1)S(1)}, u32[]{:S(2)}, u32[]{:S(2)}) %collective-permute-start.26) | collective-permute-done | bytes 393248 | tf_op jit(solution)/shard_map/ppermute | solution.py:310
  217.4 2.1 collective-permute-start.6
  219.5 6.3 %collective-permute-done.28.refs_3_ = bf16[96,2048]{1,0:T(8,128)(2,1)S(1)} collective-permute-done((bf16[96,2048]{1,0:T(8,128)(2,1)S(1)}, bf16[96,2048]{1,0:T(8,128)(2,1)S(1)}, u32[]{:S(2)}, u32[]{:S(2)}) %collective-permute-start.28) | collective-permute-done | bytes 393248 | tf_op jit(solution)/shard_map/ppermute | solution.py:310
  225.8 1.2 collective-permute-start.8
  227.0 10.5 %collective-permute-done.30.refs_4_ = bf16[96,2048]{1,0:T(8,128)(2,1)S(1)} collective-permute-done((bf16[96,2048]{1,0:T(8,128)(2,1)S(1)}, bf16[96,2048]{1,0:T(8,128)(2,1)S(1)}, u32[]{:S(2)}, u32[]{:S(2)}) %collective-permute-start.30) | collective-permute-done | bytes 393248 | tf_op jit(solution)/shard_map/ppermute | solution.py:310
  237.5 9.1 %collective-permute-done.32.refs_5_ = bf16[96,2048]{1,0:T(8,128)(2,1)S(1)} collective-permute-done((bf16[96,2048]{1,0:T(8,128)(2,1)S(1)}, bf16[96,2048]{1,0:T(8,128)(2,1)S(1)}, u32[]{:S(2)}, u32[]{:S(2)}) %collective-permute-start.32) | collective-permute-done | bytes 393248 | tf_op jit(solution)/shard_map/ppermute | solution.py:310
  246.6 1.6 unpack.2.refs_4_
  248.2 2.0 unpack.3
  (25 shorter events, 0.4 us)
Async XLA Ops:
  0.0 80.2 %collective-permute-start = (bf16[2,2048,512]{2,1,0:T(8,128)(2,1)}, bf16[2,2048,512]{2,1,0:T(8,128)(2,1)}, u32[]{:S(2)}, u32[]{:S(2)}) collective-permute-start(bf16[2,2048,512]{2,1,0:T(8,128)(2,1)} %wia.7), channel_id=1, source_target_pairs={{0,1},{1,0},{2,3},{3,2},{4,5},{5,4},{6,7},{7,6},{8,9},{9,8},{10,11... | collective-permute-start | bytes 12582920 | tf_op jit(solution)/shard_map/ppermute | solution.py:316
  0.7 80.7 %collective-permute-start.1 = (bf16[2,512,2048]{2,1,0:T(8,128)(2,1)}, bf16[2,512,2048]{2,1,0:T(8,128)(2,1)}, u32[]{:S(2)}, u32[]{:S(2)}) collective-permute-start(bf16[2,512,2048]{2,1,0:T(8,128)(2,1)} %woa.7), channel_id=1, source_target_pairs={{0,1},{1,0},{2,3},{3,2},{4,5},{5,4},{6,7},{7,6},{8,9},{9,8},{10,11... | collective-permute-start | bytes 12582920 | tf_op jit(solution)/shard_map/ppermute | solution.py:316
  0.7 0.8 copy-start.2
  1.4 0.7 copy-start.3
  4.6 10.2 %collective-permute-start.9 = (bf16[96,2048]{1,0:T(8,128)(2,1)S(1)}, bf16[96,2048]{1,0:T(8,128)(2,1)S(1)}, u32[]{:S(2)}, u32[]{:S(2)}) collective-permute-start(bf16[96,2048]{1,0:T(8,128)(2,1)S(1)} %get-tuple-element.43), channel_id=1, source_target_pairs={{0,8},{4,12},{8,0},{12,4},{16,24},{20,28},{24,16},{28,20},{1,9},{5... | collective-permute-start | bytes 1179656 | tf_op jit(solution)/shard_map/ppermute | solution.py:310
  5.6 18.9 %collective-permute-start.11 = (bf16[96,2048]{1,0:T(8,128)(2,1)S(1)}, bf16[96,2048]{1,0:T(8,128)(2,1)S(1)}, u32[]{:S(2)}, u32[]{:S(2)}) collective-permute-start(bf16[96,2048]{1,0:T(8,128)(2,1)S(1)} %get-tuple-element.46), channel_id=1, source_target_pairs={{0,24},{4,28},{8,16},{12,20},{16,8},{20,12},{24,0},{28,4},{1,25},{... | collective-permute-start | bytes 1179656 | tf_op jit(solution)/shard_map/ppermute | solution.py:310
  8.3 29.5 %collective-permute-start.15 = (bf16[96,2048]{1,0:T(8,128)(2,1)S(1)}, bf16[96,2048]{1,0:T(8,128)(2,1)S(1)}, u32[]{:S(2)}, u32[]{:S(2)}) collective-permute-start(bf16[96,2048]{1,0:T(8,128)(2,1)S(1)} %get-tuple-element.49), channel_id=1, source_target_pairs={{0,12},{4,8},{8,4},{12,0},{16,28},{20,24},{24,20},{28,16},{1,13},{... | collective-permute-start | bytes 1179656 | tf_op jit(solution)/shard_map/ppermute | solution.py:310
  14.8 50.1 %collective-permute-start.17 = (bf16[96,2048]{1,0:T(8,128)(2,1)S(1)}, bf16[96,2048]{1,0:T(8,128)(2,1)S(1)}, u32[]{:S(2)}, u32[]{:S(2)}) collective-permute-start(bf16[96,2048]{1,0:T(8,128)(2,1)S(1)} %get-tuple-element.50), channel_id=1, source_target_pairs={{0,28},{4,24},{8,20},{12,16},{16,12},{20,8},{24,4},{28,0},{1,29},{... | collective-permute-start | bytes 1179656 | tf_op jit(solution)/shard_map/ppermute | solution.py:310
  24.6 45.5 %collective-permute-start.21 = (bf16[96,2048]{1,0:T(8,128)(2,1)S(1)}, bf16[96,2048]{1,0:T(8,128)(2,1)S(1)}, u32[]{:S(2)}, u32[]{:S(2)}) collective-permute-start(bf16[96,2048]{1,0:T(8,128)(2,1)S(1)} %get-tuple-element.53), channel_id=1, source_target_pairs={{0,16},{4,20},{8,24},{12,28},{16,0},{20,4},{24,8},{28,12},{1,17},{... | collective-permute-start | bytes 1179656 | tf_op jit(solution)/shard_map/ppermute | solution.py:310
  37.8 40.7 %collective-permute-start.23 = (bf16[96,2048]{1,0:T(8,128)(2,1)S(1)}, bf16[96,2048]{1,0:T(8,128)(2,1)S(1)}, u32[]{:S(2)}, u32[]{:S(2)}) collective-permute-start(bf16[96,2048]{1,0:T(8,128)(2,1)S(1)} %get-tuple-element.54), channel_id=1, source_target_pairs={{0,20},{4,16},{8,28},{12,24},{16,4},{20,0},{24,12},{28,8},{1,21},{... | collective-permute-start | bytes 1179656 | tf_op jit(solution)/shard_map/ppermute | solution.py:310
  64.9 20.3 %collective-permute-start.10 = (bf16[96,2048]{1,0:T(8,128)(2,1)S(1)}, bf16[96,2048]{1,0:T(8,128)(2,1)S(1)}, u32[]{:S(2)}, u32[]{:S(2)}) collective-permute-start(bf16[96,2048]{1,0:T(8,128)(2,1)S(1)} %collective-permute-done.9), channel_id=1, source_target_pairs={{0,2},{1,3},{2,0},{3,1},{4,6},{5,7},{6,4},{7,5},{8,10},{9,11},{10,... | collective-permute-start | bytes 1179656 | tf_op jit(solution)/shard_map/ppermute | solution.py:313
  70.0 16.4 %collective-permute-start.12 = (bf16[96,2048]{1,0:T(8,128)(2,1)S(1)}, bf16[96,2048]{1,0:T(8,128)(2,1)S(1)}, u32[]{:S(2)}, u32[]{:S(2)}) collective-permute-start(bf16[96,2048]{1,0:T(8,128)(2,1)S(1)} %collective-permute-done.11), channel_id=1, source_target_pairs={{0,2},{1,3},{2,0},{3,1},{4,6},{5,7},{6,4},{7,5},{8,10},{9,11},{10,... | collective-permute-start | bytes 1179656 | tf_op jit(solution)/shard_map/ppermute | solution.py:313
  78.5 8.3 %copy-start = (bf16[2,2048,512]{2,1,0:T(8,128)(2,1)S(1)}, bf16[2,2048,512]{2,1,0:T(8,128)(2,1)}, u32[]{:S(2)}) copy-start(bf16[2,2048,512]{2,1,0:T(8,128)(2,1)} %wia.7) | copy-start | bytes 12582916
  78.5 8.3 %copy-start.1 = (bf16[2,512,2048]{2,1,0:T(8,128)(2,1)S(1)}, bf16[2,512,2048]{2,1,0:T(8,128)(2,1)}, u32[]{:S(2)}) copy-start(bf16[2,512,2048]{2,1,0:T(8,128)(2,1)} %woa.7) | copy-start | bytes 12582916
  78.5 12.6 %collective-permute-start.3 = (bf16[96,2048]{1,0:T(8,128)(2,1)S(1)}, bf16[96,2048]{1,0:T(8,128)(2,1)S(1)}, u32[]{:S(2)}, u32[]{:S(2)}) collective-permute-start(bf16[96,2048]{1,0:T(8,128)(2,1)S(1)} %get-tuple-element.38), channel_id=1, source_target_pairs={{0,4},{4,0},{8,12},{12,8},{16,20},{20,16},{24,28},{28,24},{1,5},{5... | collective-permute-start | bytes 1179656 | tf_op jit(solution)/shard_map/ppermute | solution.py:310
  80.2 12.1 %collective-permute-start.16 = (bf16[96,2048]{1,0:T(8,128)(2,1)S(1)}, bf16[96,2048]{1,0:T(8,128)(2,1)S(1)}, u32[]{:S(2)}, u32[]{:S(2)}) collective-permute-start(bf16[96,2048]{1,0:T(8,128)(2,1)S(1)} %collective-permute-done.15), channel_id=1, source_target_pairs={{0,2},{1,3},{2,0},{3,1},{4,6},{5,7},{6,4},{7,5},{8,10},{9,11},{10,... | collective-permute-start | bytes 1179656 | tf_op jit(solution)/shard_map/ppermute | solution.py:313
  81.4 18.4 %collective-permute-start.18 = (bf16[96,2048]{1,0:T(8,128)(2,1)S(1)}, bf16[96,2048]{1,0:T(8,128)(2,1)S(1)}, u32[]{:S(2)}, u32[]{:S(2)}) collective-permute-start(bf16[96,2048]{1,0:T(8,128)(2,1)S(1)} %collective-permute-done.17), channel_id=1, source_target_pairs={{0,2},{1,3},{2,0},{3,1},{4,6},{5,7},{6,4},{7,5},{8,10},{9,11},{10,... | collective-permute-start | bytes 1179656 | tf_op jit(solution)/shard_map/ppermute | solution.py:313
  85.2 23.0 %collective-permute-start.22 = (bf16[96,2048]{1,0:T(8,128)(2,1)S(1)}, bf16[96,2048]{1,0:T(8,128)(2,1)S(1)}, u32[]{:S(2)}, u32[]{:S(2)}) collective-permute-start(bf16[96,2048]{1,0:T(8,128)(2,1)S(1)} %collective-permute-done.21), channel_id=1, source_target_pairs={{0,2},{1,3},{2,0},{3,1},{4,6},{5,7},{6,4},{7,5},{8,10},{9,11},{10,... | collective-permute-start | bytes 1179656 | tf_op jit(solution)/shard_map/ppermute | solution.py:313
  86.5 30.2 %collective-permute-start.24 = (bf16[96,2048]{1,0:T(8,128)(2,1)S(1)}, bf16[96,2048]{1,0:T(8,128)(2,1)S(1)}, u32[]{:S(2)}, u32[]{:S(2)}) collective-permute-start(bf16[96,2048]{1,0:T(8,128)(2,1)S(1)} %collective-permute-done.23), channel_id=1, source_target_pairs={{0,2},{1,3},{2,0},{3,1},{4,6},{5,7},{6,4},{7,5},{8,10},{9,11},{10,... | collective-permute-start | bytes 1179656 | tf_op jit(solution)/shard_map/ppermute | solution.py:313
  91.1 34.0 %collective-permute-start.2 = (bf16[96,2048]{1,0:T(8,128)(2,1)S(1)}, bf16[96,2048]{1,0:T(8,128)(2,1)S(1)}, u32[]{:S(2)}, u32[]{:S(2)}) collective-permute-start(bf16[96,2048]{1,0:T(8,128)(2,1)S(1)} %get-tuple-element.37), channel_id=1, source_target_pairs={{0,2},{1,3},{2,0},{3,1},{4,6},{5,7},{6,4},{7,5},{8,10},{9,11},{10,... | collective-permute-start | bytes 1179656 | tf_op jit(solution)/shard_map/ppermute | solution.py:313
  92.3 41.1 %collective-permute-start.4 = (bf16[96,2048]{1,0:T(8,128)(2,1)S(1)}, bf16[96,2048]{1,0:T(8,128)(2,1)S(1)}, u32[]{:S(2)}, u32[]{:S(2)}) collective-permute-start(bf16[96,2048]{1,0:T(8,128)(2,1)S(1)} %collective-permute-done.3), channel_id=1, source_target_pairs={{0,2},{1,3},{2,0},{3,1},{4,6},{5,7},{6,4},{7,5},{8,10},{9,11},{10,... | collective-permute-start | bytes 1179656 | tf_op jit(solution)/shard_map/ppermute | solution.py:313
  99.8 42.1 %collective-permute-start.13 = (bf16[96,2048]{1,0:T(8,128)(2,1)S(1)}, bf16[96,2048]{1,0:T(8,128)(2,1)S(1)}, u32[]{:S(2)}, u32[]{:S(2)}) collective-permute-start(bf16[96,2048]{1,0:T(8,128)(2,1)S(1)} %bitcast.62), channel_id=1, source_target_pairs={{0,2},{1,3},{2,0},{3,1},{4,6},{5,7},{6,4},{7,5},{8,10},{9,11},{10,... | collective-permute-start | bytes 1179656 | tf_op jit(solution)/shard_map/ppermute | solution.py:313
  108.2 42.1 %collective-permute-start.19 = (bf16[96,2048]{1,0:T(8,128)(2,1)S(1)}, bf16[96,2048]{1,0:T(8,128)(2,1)S(1)}, u32[]{:S(2)}, u32[]{:S(2)}) collective-permute-start(bf16[96,2048]{1,0:T(8,128)(2,1)S(1)} %bitcast.64), channel_id=1, source_target_pairs={{0,2},{1,3},{2,0},{3,1},{4,6},{5,7},{6,4},{7,5},{8,10},{9,11},{10,... | collective-permute-start | bytes 1179656 | tf_op jit(solution)/shard_map/ppermute | solution.py:313
  121.0 37.8 %collective-permute-start.25 = (bf16[96,2048]{1,0:T(8,128)(2,1)S(1)}, bf16[96,2048]{1,0:T(8,128)(2,1)S(1)}, u32[]{:S(2)}, u32[]{:S(2)}) collective-permute-start(bf16[96,2048]{1,0:T(8,128)(2,1)S(1)} %bitcast.66), channel_id=1, source_target_pairs={{0,2},{1,3},{2,0},{3,1},{4,6},{5,7},{6,4},{7,5},{8,10},{9,11},{10,... | collective-permute-start | bytes 1179656 | tf_op jit(solution)/shard_map/ppermute | solution.py:313
  125.1 42.1 %collective-permute-start.27 = (bf16[96,2048]{1,0:T(8,128)(2,1)S(1)}, bf16[96,2048]{1,0:T(8,128)(2,1)S(1)}, u32[]{:S(2)}, u32[]{:S(2)}) collective-permute-start(bf16[96,2048]{1,0:T(8,128)(2,1)S(1)} %bitcast.65), channel_id=1, source_target_pairs={{0,2},{1,3},{2,0},{3,1},{4,6},{5,7},{6,4},{7,5},{8,10},{9,11},{10,... | collective-permute-start | bytes 1179656 | tf_op jit(solution)/shard_map/ppermute | solution.py:313
  133.5 42.1 %collective-permute-start.29 = (bf16[96,2048]{1,0:T(8,128)(2,1)S(1)}, bf16[96,2048]{1,0:T(8,128)(2,1)S(1)}, u32[]{:S(2)}, u32[]{:S(2)}) collective-permute-start(bf16[96,2048]{1,0:T(8,128)(2,1)S(1)} %bitcast.59), channel_id=1, source_target_pairs={{0,2},{1,3},{2,0},{3,1},{4,6},{5,7},{6,4},{7,5},{8,10},{9,11},{10,... | collective-permute-start | bytes 1179656 | tf_op jit(solution)/shard_map/ppermute | solution.py:313
  141.9 42.1 %collective-permute-start.31 = (bf16[96,2048]{1,0:T(8,128)(2,1)S(1)}, bf16[96,2048]{1,0:T(8,128)(2,1)S(1)}, u32[]{:S(2)}, u32[]{:S(2)}) collective-permute-start(bf16[96,2048]{1,0:T(8,128)(2,1)S(1)} %bitcast.61), channel_id=1, source_target_pairs={{0,2},{1,3},{2,0},{3,1},{4,6},{5,7},{6,4},{7,5},{8,10},{9,11},{10,... | collective-permute-start | bytes 1179656 | tf_op jit(solution)/shard_map/ppermute | solution.py:313
  150.3 35.5 %collective-permute-start.7 = (bf16[96,2048]{1,0:T(8,128)(2,1)S(1)}, bf16[96,2048]{1,0:T(8,128)(2,1)S(1)}, u32[]{:S(2)}, u32[]{:S(2)}) collective-permute-start(bf16[96,2048]{1,0:T(8,128)(2,1)S(1)} %bitcast.63), channel_id=1, source_target_pairs={{0,4},{4,0},{8,12},{12,8},{16,20},{20,16},{24,28},{28,24},{1,5},{5... | collective-permute-start | bytes 1179656 | tf_op jit(solution)/shard_map/ppermute | solution.py:310
  158.8 28.6 %collective-permute-start.14 = (bf16[96,2048]{1,0:T(8,128)(2,1)S(1)}, bf16[96,2048]{1,0:T(8,128)(2,1)S(1)}, u32[]{:S(2)}, u32[]{:S(2)}) collective-permute-start(bf16[96,2048]{1,0:T(8,128)(2,1)S(1)} %add.6), channel_id=1, source_target_pairs={{0,8},{4,12},{8,0},{12,4},{16,24},{20,28},{24,16},{28,20},{1,9},{5... | collective-permute-start | bytes 1179656 | tf_op jit(solution)/shard_map/ppermute | solution.py:310
  167.2 20.2 %collective-permute-start.20 = (bf16[96,2048]{1,0:T(8,128)(2,1)S(1)}, bf16[96,2048]{1,0:T(8,128)(2,1)S(1)}, u32[]{:S(2)}, u32[]{:S(2)}) collective-permute-start(bf16[96,2048]{1,0:T(8,128)(2,1)S(1)} %add.7), channel_id=1, source_target_pairs={{0,12},{4,8},{8,4},{12,0},{16,28},{20,24},{24,20},{28,16},{1,13},{... | collective-permute-start | bytes 1179656 | tf_op jit(solution)/shard_map/ppermute | solution.py:310
  175.6 41.8 %collective-permute-start.26 = (bf16[96,2048]{1,0:T(8,128)(2,1)S(1)}, bf16[96,2048]{1,0:T(8,128)(2,1)S(1)}, u32[]{:S(2)}, u32[]{:S(2)}) collective-permute-start(bf16[96,2048]{1,0:T(8,128)(2,1)S(1)} %add.8), channel_id=1, source_target_pairs={{0,16},{4,20},{8,24},{12,28},{16,0},{20,4},{24,8},{28,12},{1,17},{... | collective-permute-start | bytes 1179656 | tf_op jit(solution)/shard_map/ppermute | solution.py:310
  184.0 41.8 %collective-permute-start.28 = (bf16[96,2048]{1,0:T(8,128)(2,1)S(1)}, bf16[96,2048]{1,0:T(8,128)(2,1)S(1)}, u32[]{:S(2)}, u32[]{:S(2)}) collective-permute-start(bf16[96,2048]{1,0:T(8,128)(2,1)S(1)} %add.9), channel_id=1, source_target_pairs={{0,20},{4,16},{8,28},{12,24},{16,4},{20,0},{24,12},{28,8},{1,21},{... | collective-permute-start | bytes 1179656 | tf_op jit(solution)/shard_map/ppermute | solution.py:310
  185.9 51.6 %collective-permute-start.30 = (bf16[96,2048]{1,0:T(8,128)(2,1)S(1)}, bf16[96,2048]{1,0:T(8,128)(2,1)S(1)}, u32[]{:S(2)}, u32[]{:S(2)}) collective-permute-start(bf16[96,2048]{1,0:T(8,128)(2,1)S(1)} %add.10), channel_id=1, source_target_pairs={{0,24},{4,28},{8,16},{12,20},{16,8},{20,12},{24,0},{28,4},{1,25},{... | collective-permute-start | bytes 1179656 | tf_op jit(solution)/shard_map/ppermute | solution.py:310
  187.3 59.3 %collective-permute-start.32 = (bf16[96,2048]{1,0:T(8,128)(2,1)S(1)}, bf16[96,2048]{1,0:T(8,128)(2,1)S(1)}, u32[]{:S(2)}, u32[]{:S(2)}) collective-permute-start(bf16[96,2048]{1,0:T(8,128)(2,1)S(1)} %add.11), channel_id=1, source_target_pairs={{0,28},{4,24},{8,20},{12,16},{16,12},{20,8},{24,4},{28,0},{1,29},{... | collective-permute-start | bytes 1179656 | tf_op jit(solution)/shard_map/ppermute | solution.py:310
  187.3 60.8 %collective-permute-start.5 = (bf16[96,2048]{1,0:T(8,128)(2,1)S(1)}, bf16[96,2048]{1,0:T(8,128)(2,1)S(1)}, u32[]{:S(2)}, u32[]{:S(2)}) collective-permute-start(bf16[96,2048]{1,0:T(8,128)(2,1)S(1)} %bitcast.60), channel_id=1, source_target_pairs={{0,2},{1,3},{2,0},{3,1},{4,6},{5,7},{6,4},{7,5},{8,10},{9,11},{10,... | collective-permute-start | bytes 1179656 | tf_op jit(solution)/shard_map/ppermute | solution.py:313
  217.4 30.8 %collective-permute-start.6 = (bf16[96,2048]{1,0:T(8,128)(2,1)S(1)}, bf16[96,2048]{1,0:T(8,128)(2,1)S(1)}, u32[]{:S(2)}, u32[]{:S(2)}) collective-permute-start(bf16[96,2048]{1,0:T(8,128)(2,1)S(1)} %bitcast.58), channel_id=1, source_target_pairs={{0,4},{4,0},{8,12},{12,8},{16,20},{20,16},{24,28},{28,24},{1,5},{5... | collective-permute-start | bytes 1179656 | tf_op jit(solution)/shard_map/ppermute | solution.py:310
  225.8 22.4 %collective-permute-start.8 = (bf16[96,2048]{1,0:T(8,128)(2,1)S(1)}, bf16[96,2048]{1,0:T(8,128)(2,1)S(1)}, u32[]{:S(2)}, u32[]{:S(2)}) collective-permute-start(bf16[96,2048]{1,0:T(8,128)(2,1)S(1)} %collective-permute-done.7), channel_id=1, source_target_pairs={{0,2},{1,3},{2,0},{3,1},{4,6},{5,7},{6,4},{7,5},{8,10},{9,11},{10,... | collective-permute-start | bytes 1179656 | tf_op jit(solution)/shard_map/ppermute | solution.py:313
